TPU v7x, 128 devices: a whole 4x4x4 slice. The times are simulated.
128 devices in a mesh: seq: 4 (over z_lo, core), mp: 32 (over z_hi, y, x).
Axes of the slice: x: 4, y: 4, z: 4 (z_hi: 2, z_lo: 2; z = z_hi * 2 + z_lo), core: 2. Of those that a mesh axis runs over, the one named last changes fastest.
Arguments:
- byte_states: bfloat16 [4, 16384, 1024], P('seq', 'mp'), may hold values from -312 to 312
- patch_latents: bfloat16 [4, 4096, 4096], P(None, 'seq', 'mp'), may hold values from -6 to 6
- patch_lengths: int32 [4, 4096], P('seq'), may hold values from 1 to 12, 16384 in all within a row
- w_down: bfloat16 [4096, 1024], replicated, may hold values from -0.09375 to 0.09375
- kv_gain: bfloat16 [1024], replicated, may hold values from 0.25 to 1.75
- w_query: bfloat16 [1024, 1024], replicated, may hold values from -0.375 to 0.375
- w_key: bfloat16 [1024, 1024], replicated, may hold values from -0.1875 to 0.1875
- w_value: bfloat16 [1024, 1024], replicated, may hold values from -0.1875 to 0.1875
- w_out: bfloat16 [1024, 1024], replicated, may hold values from -0.375 to 0.375
- out_gain: bfloat16 [1024], replicated, may hold values from 0.25 to 1.75
Outputs:
- decoded: bfloat16 [4, 16384, 1024], P('seq', 'mp')
Inputs may be any that keep to these rules, and one draw needn't show every extreme that they name: patch_lengths[s] lists the lengths of the 4096 patches of sequence s in order; they sum to 16384 and the longest is exactly 12.
All inputs are finite; a program needn't handle non-finite values.
Results may differ from a plain program's by a relative error of at most 0.0076.
Values may be sent and summed in bfloat16 or wider, within the bound.
No kernel may reach another device: no remote copies, remote signals or barrier semaphores. Data moves between devices by JAX's collectives and lax.ppermute only.
A program may use at most 128 MiB of HBM per device.

v0:
```python
import math

import jax
import jax.numpy as jnp
from jax import lax
from jax.sharding import PartitionSpec as P

HEADS = 16
HEAD_DIM = 64


NEG_FLOOR = -1e30


def from_partner(value, axis, apart):
    mask = 2**apart
    pairs = [(source, source ^ mask) for source in range(lax.axis_size(axis))]
    return lax.ppermute(value, axis, pairs)


def in_one_piece(arrays, axis, dim, along):
    both = jnp.concatenate(arrays, axis=along)
    filled, at, finished = (lax.all_gather(both, axis, axis=dim, tiled=True), 0, [])
    for a in arrays:
        finished.append(lax.slice_in_dim(filled, at, at + a.shape[along], axis=along))
        at += a.shape[along]
    return tuple(finished)


def rms_norm(values, gain_row):
    mean_square = jnp.mean(values * values, axis=-1, keepdims=True)
    return values * lax.rsqrt(mean_square + 1e-05) * gain_row.astype(jnp.float32)


def fold_block(fold_state, query_part, position_part, key_block, value_block, start_block):
    row_max, denominator, accumulated = fold_state
    scale_factor = 1.0 / math.sqrt(HEAD_DIM)
    scores = (
        jnp.einsum("rhd,khd->hrk", query_part, key_block, preferred_element_type=jnp.float32)
        * scale_factor
    )
    allowed = start_block[None, None, :] <= position_part[None, :, None]
    masked = jnp.where(allowed, scores, NEG_FLOOR)
    new_max = jnp.maximum(row_max, jnp.max(masked, axis=-1))
    raised = jnp.where(allowed, jnp.exp(masked - new_max[..., None]), 0.0)
    correction = jnp.exp(row_max - new_max)
    denominator = denominator * correction + jnp.sum(raised, axis=-1)
    accumulated = accumulated * correction[..., None] + jnp.einsum(
        "hrk,khd->hrd", raised.astype(jnp.bfloat16), value_block, preferred_element_type=jnp.float32
    )
    return (new_max, denominator, accumulated)


def make_folder(query_halves, position_halves, starts):

    def folder(running, arrived_piece, piece_start):
        key_piece, value_piece = arrived_piece
        piece_rows = key_piece.shape[0]
        step_rows = math.gcd(piece_rows, 512)

        def one_block(block_index, fold_state):
            offset = block_index * step_rows
            key_block = lax.dynamic_slice_in_dim(key_piece, offset, step_rows, 0).reshape(
                step_rows, HEADS, HEAD_DIM
            )
            value_block = lax.dynamic_slice_in_dim(value_piece, offset, step_rows, 0).reshape(
                step_rows, HEADS, HEAD_DIM
            )
            start_block = lax.dynamic_slice_in_dim(starts, offset, step_rows, 0)
            updated = []
            for part_index in range(2):
                part_state = tuple((member[part_index] for member in fold_state))

                def advance(inner_state, part_index=part_index):
                    return fold_block(
                        inner_state,
                        query_halves[part_index],
                        position_halves[part_index],
                        key_block,
                        value_block,
                        start_block,
                    )

                def remain(inner_state):
                    return inner_state

                needed = start_block[0] <= position_halves[part_index][-1]
                updated.append(lax.cond(needed, advance, remain, part_state))
            return tuple((jnp.stack([updated[0][slot], updated[1][slot]]) for slot in range(3)))

        return lax.fori_loop(0, piece_rows // step_rows, one_block, running)

    return folder


def per_device(
    byte_states,
    patch_latents,
    patch_lengths,
    w_down,
    kv_gain,
    w_query,
    w_key,
    w_value,
    w_out,
    out_gain,
):
    mp_count = lax.axis_size("mp")
    my_rank = lax.axis_index("mp")
    tokens_here = byte_states.shape[1]
    half_rows = tokens_here // 2
    regrouped = lax.all_to_all(
        lax.all_to_all(patch_latents, "seq", split_axis=0, concat_axis=1, tiled=True),
        "mp",
        split_axis=1,
        concat_axis=2,
        tiled=True,
    )
    projected = jnp.dot(regrouped[0], w_down, preferred_element_type=jnp.float32)
    patch_normed = rms_norm(projected, kv_gain).astype(jnp.bfloat16)
    lengths = patch_lengths[0]
    starts = jnp.cumsum(lengths) - lengths
    own_rows = byte_states[0]
    local_offsets = jnp.arange(half_rows, dtype=jnp.int32)
    first_position = my_rank * tokens_here
    top_bit = mp_count.bit_length() - 2
    partner = jnp.bitwise_xor(my_rank, mp_count // 2)
    arrived_rows = from_partner(own_rows[half_rows:], "mp", top_bit)
    work_rows = jnp.concatenate([own_rows[:half_rows], arrived_rows], axis=0)
    position_halves = jnp.stack(
        [first_position + local_offsets, partner * tokens_here + half_rows + local_offsets]
    )
    queries = jnp.dot(work_rows, w_query, preferred_element_type=jnp.float32).astype(jnp.bfloat16)
    query_halves = queries.reshape(2, half_rows, HEADS, HEAD_DIM)
    initial = (
        jnp.full((2, HEADS, half_rows), NEG_FLOOR, jnp.float32),
        jnp.zeros((2, HEADS, half_rows), jnp.float32),
        jnp.zeros((2, HEADS, half_rows, HEAD_DIM), jnp.float32),
    )
    key_rows = jnp.dot(patch_normed, w_key, preferred_element_type=jnp.float32).astype(jnp.bfloat16)
    value_rows = jnp.dot(patch_normed, w_value, preferred_element_type=jnp.float32).astype(
        jnp.bfloat16
    )
    folder = make_folder(query_halves, position_halves, starts)
    row_max, denominator, accumulated = folder(
        initial, in_one_piece((key_rows, value_rows), "mp", 0, 1), jnp.int32(0)
    )
    summed = accumulated / denominator[..., None]
    head_out = (
        jnp.transpose(summed, (0, 2, 1, 3))
        .reshape(tokens_here, HEADS * HEAD_DIM)
        .astype(jnp.bfloat16)
    )
    residual = work_rows.astype(jnp.float32) + jnp.dot(
        head_out, w_out, preferred_element_type=jnp.float32
    )
    decoded = rms_norm(residual, out_gain).astype(jnp.bfloat16)
    returned = from_partner(decoded[half_rows:], "mp", top_bit)
    decoded = jnp.concatenate([decoded[:half_rows], returned], axis=0)
    return decoded[None]


def solution(mesh):
    return jax.shard_map(
        per_device,
        mesh=mesh,
        in_specs=(
            P("seq", "mp", None),
            P(None, "seq", "mp"),
            P("seq", None),
            P(),
            P(),
            P(),
            P(),
            P(),
            P(),
            P(),
        ),
        out_specs=P("seq", "mp", None),
        check_vma=False,
    )
```

profile of v0, /device:TPU:24, one launch (start us, length us, event | category | flops | bytes accessed | tf_op | source)
XLA Modules:
  0.0 601.6 jit_solution(1319241090054931026)
XLA Ops:
  6.5 18.0 %all_to_all.27 = bf16[4,1024,128]{2,1,0:T(8,128)(2,1)S(1)} all-to-all(bf16[4,1024,128]{2,1,0:T(8,128)(2,1)} %param.17), channel_id=1, replica_groups=mesh['seq'=4,'mp'=32] {'seq'}, dimensions={0} | all-to-all | bytes 2097152 | tf_op jit(solution)/shard_map/all_to_all | solution.py:113
  24.6 17.0 %copy.45 = bf16[1,4096,128]{2,0,1:T(2,128)(2,1)} copy(bf16[1,4096,128]{2,1,0:T(8,128)(2,1)S(1)} %bitcast.101) | data formatting | bytes 2097152 | tf_op jit(solution)/shard_map/all_to_all | solution.py:113
  42.1 23.4 %reduce.2 = bf16[4096,128]{1,0:T(8,128)(2,1)S(1)} reduce(bf16[4096,1,128]{2,1,0:T(2,128)(2,1)} %bitcast.98, bf16[]{:T(256)} %broadcast.104), dimensions={1}, to_apply=%bitcast.78.reduce_sub_computation | reduce | bytes 2097154
  66.7 10.6 %all-to-all-start.1 = ((bf16[32,2,8192]{2,1,0:T(2,128)(2,1)}), bf16[32,2,8192]{2,1,0:T(2,128)(2,1)S(1)}, u32[]{:S(2)}, u32[]{:S(2)}) async-start(bf16[32,2,8192]{2,1,0:T(2,128)(2,1)} %reshape.140), calls=%async_computation.1 | async-start | bytes 2097152 | tf_op jit(solution)/shard_map/all_to_all | solution.py:112
  77.5 16.8 %all-to-all-done.1 = bf16[32,2,8192]{2,1,0:T(2,128)(2,1)S(1)} async-done(((bf16[32,2,8192]{2,1,0:T(2,128)(2,1)}), bf16[32,2,8192]{2,1,0:T(2,128)(2,1)S(1)}, u32[]{:S(2)}, u32[]{:S(2)}) %all-to-all-start.1) | async-done | bytes 1048608 | tf_op jit(solution)/shard_map/all_to_all | solution.py:112
  102.2 4.9 multiply_reduce_fusion.1
  112.3 15.8 %collective-permute-done = bf16[256,1024]{1,0:T(8,128)(2,1)S(1)} collective-permute-done((bf16[256,1024]{1,0:T(8,128)(2,1)}, bf16[256,1024]{1,0:T(8,128)(2,1)S(1)}, u32[]{:S(2)}, u32[]{:S(2)}) %collective-permute-start) | collective-permute-done | bytes 524320 | tf_op jit(solution)/shard_map/ppermute | solution.py:18
  132.1 4.0 reshape.138
  139.6 123.1 %all-gather.2.cloned.1.call-done = bf16[4096,2048]{1,0:T(8,128)(2,1)} async-done(((bf16[128,2048]{1,0:T(8,128)(2,1)}), bf16[4096,2048]{1,0:T(8,128)(2,1)}) %all-gather.2.cloned.1.call-update) | async-done | bytes 16777232 | tf_op jit(solution)/shard_map/all_gather | solution.py:23
  262.7 11.6 %fusion.38 = (bf16[4096,1024]{1,0:T(8,128)(2,1)}, bf16[4096,1024]{1,0:T(8,128)(2,1)}) fusion(bf16[4096,2048]{1,0:T(8,128)(2,1)} %all-gather.2.cloned.1.call-done), kind=kLoop, calls=%fused_computation.69 | loop fusion | bytes 33554432 | tf_op jit(solution)/shard_map/slice | solution.py:25
  275.9 297.0 %while.17 = (s32[]{:T(128)}, f32[2,16,256]{2,1,0:T(8,128)S(1)}, f32[2,16,256]{2,1,0:T(8,128)S(1)}, f32[2,16,256,64]{2,3,1,0:T(8,128)}, s32[4096]{0:T(1024)S(1)},...) while((s32[]{:T(128)}, f32[2,16,256]{2,1,0:T(8,128)S(1)}, ...), condition=%wide.region_12.13_spmd, body=%wide.region_3.12_spmd.sunk | while | flops 1130135552 | bytes 99363408 | solution.py:91
  289.4 10.8 %conditional.5 = (f32[1,16,256]{2,1,0:T(8,128)}, f32[1,16,256]{2,1,0:T(8,128)S(1)}, f32[1,16,256,64]{2,3,1,0:T(8,128)S(1)}) conditional(s32[]{:T(128)} %bitcast.90, (f32[16,256]{1,0:T(8,128)}, f32[16,256]{1,0:T(8,128)S(1)}, f32[16,256,64]{1,2,0:T(8,128)S(1)}) %tuple.134, (s32[512]{0:T(512)S(1)}, s32[256]{0:T(256)S(1)}, ...), branch_computations={%region_4.4_spmd, %region_5.0_spmd} | conditional | flops 564797440 | bytes 34835508 | solution.py:88
  302.8 11.9 %conditional.4 = (f32[1,16,256]{2,1,0:T(8,128)}, f32[1,16,256]{2,1,0:T(8,128)S(1)}, f32[1,16,256,64]{2,3,1,0:T(8,128)}) conditional(s32[]{:T(128)} %bitcast.87, (f32[16,256]{1,0:T(8,128)}, f32[16,256]{1,0:T(8,128)S(1)}, f32[16,256,64]{1,2,0:T(8,128)}) %tuple.132, (s32[512]{0:T(512)S(1)}, s32[256]{0:T(256)S(1)}, bf16[2,256,16,64]{1,3,2,0:T(8,128)(2,1)}, ...), branch_computations={%region_8.8_spmd, %region_9.0_spmd} | conditional | flops 564797440 | bytes 43224172 | solution.py:88
  331.9 10.8 %conditional.5 = (f32[1,16,256]{2,1,0:T(8,128)}, f32[1,16,256]{2,1,0:T(8,128)S(1)}, f32[1,16,256,64]{2,3,1,0:T(8,128)S(1)}) conditional(s32[]{:T(128)} %bitcast.90, (f32[16,256]{1,0:T(8,128)}, f32[16,256]{1,0:T(8,128)S(1)}, f32[16,256,64]{1,2,0:T(8,128)S(1)}) %tuple.134, (s32[512]{0:T(512)S(1)}, s32[256]{0:T(256)S(1)}, ...), branch_computations={%region_4.4_spmd, %region_5.0_spmd} | conditional | flops 564797440 | bytes 34835508 | solution.py:88
  345.3 11.9 %conditional.4 = (f32[1,16,256]{2,1,0:T(8,128)}, f32[1,16,256]{2,1,0:T(8,128)S(1)}, f32[1,16,256,64]{2,3,1,0:T(8,128)}) conditional(s32[]{:T(128)} %bitcast.87, (f32[16,256]{1,0:T(8,128)}, f32[16,256]{1,0:T(8,128)S(1)}, f32[16,256,64]{1,2,0:T(8,128)}) %tuple.132, (s32[512]{0:T(512)S(1)}, s32[256]{0:T(256)S(1)}, bf16[2,256,16,64]{1,3,2,0:T(8,128)(2,1)}, ...), branch_computations={%region_8.8_spmd, %region_9.0_spmd} | conditional | flops 564797440 | bytes 43224172 | solution.py:88
  374.4 10.8 %conditional.5 = (f32[1,16,256]{2,1,0:T(8,128)}, f32[1,16,256]{2,1,0:T(8,128)S(1)}, f32[1,16,256,64]{2,3,1,0:T(8,128)S(1)}) conditional(s32[]{:T(128)} %bitcast.90, (f32[16,256]{1,0:T(8,128)}, f32[16,256]{1,0:T(8,128)S(1)}, f32[16,256,64]{1,2,0:T(8,128)S(1)}) %tuple.134, (s32[512]{0:T(512)S(1)}, s32[256]{0:T(256)S(1)}, ...), branch_computations={%region_4.4_spmd, %region_5.0_spmd} | conditional | flops 564797440 | bytes 34835508 | solution.py:88
  387.8 11.9 %conditional.4 = (f32[1,16,256]{2,1,0:T(8,128)}, f32[1,16,256]{2,1,0:T(8,128)S(1)}, f32[1,16,256,64]{2,3,1,0:T(8,128)}) conditional(s32[]{:T(128)} %bitcast.87, (f32[16,256]{1,0:T(8,128)}, f32[16,256]{1,0:T(8,128)S(1)}, f32[16,256,64]{1,2,0:T(8,128)}) %tuple.132, (s32[512]{0:T(512)S(1)}, s32[256]{0:T(256)S(1)}, bf16[2,256,16,64]{1,3,2,0:T(8,128)(2,1)}, ...), branch_computations={%region_8.8_spmd, %region_9.0_spmd} | conditional | flops 564797440 | bytes 43224172 | solution.py:88
  416.9 10.8 %conditional.5 = (f32[1,16,256]{2,1,0:T(8,128)}, f32[1,16,256]{2,1,0:T(8,128)S(1)}, f32[1,16,256,64]{2,3,1,0:T(8,128)S(1)}) conditional(s32[]{:T(128)} %bitcast.90, (f32[16,256]{1,0:T(8,128)}, f32[16,256]{1,0:T(8,128)S(1)}, f32[16,256,64]{1,2,0:T(8,128)S(1)}) %tuple.134, (s32[512]{0:T(512)S(1)}, s32[256]{0:T(256)S(1)}, ...), branch_computations={%region_4.4_spmd, %region_5.0_spmd} | conditional | flops 564797440 | bytes 34835508 | solution.py:88
  430.3 11.9 %conditional.4 = (f32[1,16,256]{2,1,0:T(8,128)}, f32[1,16,256]{2,1,0:T(8,128)S(1)}, f32[1,16,256,64]{2,3,1,0:T(8,128)}) conditional(s32[]{:T(128)} %bitcast.87, (f32[16,256]{1,0:T(8,128)}, f32[16,256]{1,0:T(8,128)S(1)}, f32[16,256,64]{1,2,0:T(8,128)}) %tuple.132, (s32[512]{0:T(512)S(1)}, s32[256]{0:T(256)S(1)}, bf16[2,256,16,64]{1,3,2,0:T(8,128)(2,1)}, ...), branch_computations={%region_8.8_spmd, %region_9.0_spmd} | conditional | flops 564797440 | bytes 43224172 | solution.py:88
  462.0 11.9 %conditional.4 = (f32[1,16,256]{2,1,0:T(8,128)}, f32[1,16,256]{2,1,0:T(8,128)S(1)}, f32[1,16,256,64]{2,3,1,0:T(8,128)}) conditional(s32[]{:T(128)} %bitcast.87, (f32[16,256]{1,0:T(8,128)}, f32[16,256]{1,0:T(8,128)S(1)}, f32[16,256,64]{1,2,0:T(8,128)}) %tuple.132, (s32[512]{0:T(512)S(1)}, s32[256]{0:T(256)S(1)}, bf16[2,256,16,64]{1,3,2,0:T(8,128)(2,1)}, ...), branch_computations={%region_8.8_spmd, %region_9.0_spmd} | conditional | flops 564797440 | bytes 43224172 | solution.py:88
  493.7 11.9 %conditional.4 = (f32[1,16,256]{2,1,0:T(8,128)}, f32[1,16,256]{2,1,0:T(8,128)S(1)}, f32[1,16,256,64]{2,3,1,0:T(8,128)}) conditional(s32[]{:T(128)} %bitcast.87, (f32[16,256]{1,0:T(8,128)}, f32[16,256]{1,0:T(8,128)S(1)}, f32[16,256,64]{1,2,0:T(8,128)}) %tuple.132, (s32[512]{0:T(512)S(1)}, s32[256]{0:T(256)S(1)}, bf16[2,256,16,64]{1,3,2,0:T(8,128)(2,1)}, ...), branch_computations={%region_8.8_spmd, %region_9.0_spmd} | conditional | flops 564797440 | bytes 43224172 | solution.py:88
  525.5 11.9 %conditional.4 = (f32[1,16,256]{2,1,0:T(8,128)}, f32[1,16,256]{2,1,0:T(8,128)S(1)}, f32[1,16,256,64]{2,3,1,0:T(8,128)}) conditional(s32[]{:T(128)} %bitcast.87, (f32[16,256]{1,0:T(8,128)}, f32[16,256]{1,0:T(8,128)S(1)}, f32[16,256,64]{1,2,0:T(8,128)}) %tuple.132, (s32[512]{0:T(512)S(1)}, s32[256]{0:T(256)S(1)}, bf16[2,256,16,64]{1,3,2,0:T(8,128)(2,1)}, ...), branch_computations={%region_8.8_spmd, %region_9.0_spmd} | conditional | flops 564797440 | bytes 43224172 | solution.py:88
  557.2 11.9 %conditional.4 = (f32[1,16,256]{2,1,0:T(8,128)}, f32[1,16,256]{2,1,0:T(8,128)S(1)}, f32[1,16,256,64]{2,3,1,0:T(8,128)}) conditional(s32[]{:T(128)} %bitcast.87, (f32[16,256]{1,0:T(8,128)}, f32[16,256]{1,0:T(8,128)S(1)}, f32[16,256,64]{1,2,0:T(8,128)}) %tuple.132, (s32[512]{0:T(512)S(1)}, s32[256]{0:T(256)S(1)}, bf16[2,256,16,64]{1,3,2,0:T(8,128)(2,1)}, ...), branch_computations={%region_8.8_spmd, %region_9.0_spmd} | conditional | flops 564797440 | bytes 43224172 | solution.py:88
  579.3 14.4 %collective-permute-done.1 = bf16[256,1024]{1,0:T(8,128)(2,1)S(1)} collective-permute-done((bf16[256,1024]{1,0:T(8,128)(2,1)S(1)}, bf16[256,1024]{1,0:T(8,128)(2,1)S(1)}, u32[]{:S(2)}, u32[]{:S(2)}) %collective-permute-start.1) | collective-permute-done | bytes 524320 | tf_op jit(solution)/shard_map/ppermute | solution.py:18
  (315 shorter events, 306.8 us)
Async XLA Ops:
  6.5 569.6 %copy-start = (bf16[1024,1024]{1,0:T(8,128)(2,1)S(1)}, bf16[1024,1024]{1,0:T(8,128)(2,1)}, u32[]{:S(2)}) copy-start(bf16[1024,1024]{1,0:T(8,128)(2,1)} %param.24) | copy-start | bytes 6291460
  6.5 71.0 %copy-start.13 = (bf16[1024]{0:T(1024)(128)(2,1)S(1)}, bf16[1024]{0:T(1024)(128)(2,1)}, u32[]{:S(2)}) copy-start(bf16[1024]{0:T(1024)(128)(2,1)} %param.20) | copy-start | bytes 6148
  66.7 27.7 %all-to-all-start.1 = ((bf16[32,2,8192]{2,1,0:T(2,128)(2,1)}), bf16[32,2,8192]{2,1,0:T(2,128)(2,1)S(1)}, u32[]{:S(2)}, u32[]{:S(2)}) async-start(bf16[32,2,8192]{2,1,0:T(2,128)(2,1)} %reshape.140), calls=%async_computation.1 | async-start | bytes 2097152 | tf_op jit(solution)/shard_map/all_to_all | solution.py:112
  77.3 185.4 %all-gather.2.cloned.1.call-start = ((), (), s32[]{:S(2)}) async-start(), calls=%async_computation.2 | async-start | bytes 17301504 | tf_op jit(solution)/shard_map/all_gather | solution.py:23
  111.1 28.5 %copy-start.6 = (bf16[256,1024]{1,0:T(8,128)(2,1)}, bf16[256,1024]{1,0:T(8,128)(2,1)S(1)}, u32[]{:S(2)}) copy-start(bf16[256,1024]{1,0:T(8,128)(2,1)S(1)} %get-tuple-element.383) | copy-start | bytes 1572868
  111.1 17.0 %collective-permute-start = (bf16[256,1024]{1,0:T(8,128)(2,1)}, bf16[256,1024]{1,0:T(8,128)(2,1)S(1)}, u32[]{:S(2)}, u32[]{:S(2)}) collective-permute-start(bf16[256,1024]{1,0:T(8,128)(2,1)} %get-tuple-element.384), channel_id=1, source_target_pairs={{0,16},{1,17},{2,18},{3,19},{4,20},{5,21},{6,22},{7,23},{8,24},{9,... | collective-permute-start | bytes 1572872 | tf_op jit(solution)/shard_map/ppermute | solution.py:18
  128.1 146.3 %copy-start.8 = (bf16[256,1024]{1,0:T(8,128)(2,1)}, bf16[256,1024]{1,0:T(8,128)(2,1)S(1)}, u32[]{:S(2)}) copy-start(bf16[256,1024]{1,0:T(8,128)(2,1)S(1)} %collective-permute-done) | copy-start | bytes 1572868
  302.9 7.5 %copy-start.1 = (f32[16,256,64]{1,2,0:T(8,128)S(1)}, f32[16,256,64]{1,2,0:T(8,128)}, u32[]{:S(2)}) copy-start(f32[16,256,64]{1,2,0:T(8,128)} %get-tuple-element.256) | copy-start | bytes 3145732 | tf_op jit(solution)/shard_map/while/body/eval_jaxpr/cond
  302.9 7.5 %copy-start.5 = (bf16[512,16,64]{0,2,1:T(8,128)(2,1)S(1)}, bf16[512,16,64]{0,2,1:T(8,128)(2,1)}, u32[]{:S(2)}) copy-start(bf16[512,16,64]{0,2,1:T(8,128)(2,1)} %get-tuple-element.257) | copy-start | bytes 3145732 | tf_op jit(solution)/shard_map/while/body/eval_jaxpr/cond
  345.4 7.5 %copy-start.1 = (f32[16,256,64]{1,2,0:T(8,128)S(1)}, f32[16,256,64]{1,2,0:T(8,128)}, u32[]{:S(2)}) copy-start(f32[16,256,64]{1,2,0:T(8,128)} %get-tuple-element.256) | copy-start | bytes 3145732 | tf_op jit(solution)/shard_map/while/body/eval_jaxpr/cond
  345.4 7.5 %copy-start.5 = (bf16[512,16,64]{0,2,1:T(8,128)(2,1)S(1)}, bf16[512,16,64]{0,2,1:T(8,128)(2,1)}, u32[]{:S(2)}) copy-start(bf16[512,16,64]{0,2,1:T(8,128)(2,1)} %get-tuple-element.257) | copy-start | bytes 3145732 | tf_op jit(solution)/shard_map/while/body/eval_jaxpr/cond
  387.9 7.5 %copy-start.1 = (f32[16,256,64]{1,2,0:T(8,128)S(1)}, f32[16,256,64]{1,2,0:T(8,128)}, u32[]{:S(2)}) copy-start(f32[16,256,64]{1,2,0:T(8,128)} %get-tuple-element.256) | copy-start | bytes 3145732 | tf_op jit(solution)/shard_map/while/body/eval_jaxpr/cond
  387.9 7.5 %copy-start.5 = (bf16[512,16,64]{0,2,1:T(8,128)(2,1)S(1)}, bf16[512,16,64]{0,2,1:T(8,128)(2,1)}, u32[]{:S(2)}) copy-start(bf16[512,16,64]{0,2,1:T(8,128)(2,1)} %get-tuple-element.257) | copy-start | bytes 3145732 | tf_op jit(solution)/shard_map/while/body/eval_jaxpr/cond
  430.4 7.5 %copy-start.1 = (f32[16,256,64]{1,2,0:T(8,128)S(1)}, f32[16,256,64]{1,2,0:T(8,128)}, u32[]{:S(2)}) copy-start(f32[16,256,64]{1,2,0:T(8,128)} %get-tuple-element.256) | copy-start | bytes 3145732 | tf_op jit(solution)/shard_map/while/body/eval_jaxpr/cond
  430.4 7.5 %copy-start.5 = (bf16[512,16,64]{0,2,1:T(8,128)(2,1)S(1)}, bf16[512,16,64]{0,2,1:T(8,128)(2,1)}, u32[]{:S(2)}) copy-start(bf16[512,16,64]{0,2,1:T(8,128)(2,1)} %get-tuple-element.257) | copy-start | bytes 3145732 | tf_op jit(solution)/shard_map/while/body/eval_jaxpr/cond
  462.2 7.5 %copy-start.1 = (f32[16,256,64]{1,2,0:T(8,128)S(1)}, f32[16,256,64]{1,2,0:T(8,128)}, u32[]{:S(2)}) copy-start(f32[16,256,64]{1,2,0:T(8,128)} %get-tuple-element.256) | copy-start | bytes 3145732 | tf_op jit(solution)/shard_map/while/body/eval_jaxpr/cond
  462.2 7.5 %copy-start.5 = (bf16[512,16,64]{0,2,1:T(8,128)(2,1)S(1)}, bf16[512,16,64]{0,2,1:T(8,128)(2,1)}, u32[]{:S(2)}) copy-start(bf16[512,16,64]{0,2,1:T(8,128)(2,1)} %get-tuple-element.257) | copy-start | bytes 3145732 | tf_op jit(solution)/shard_map/while/body/eval_jaxpr/cond
  493.9 7.5 %copy-start.1 = (f32[16,256,64]{1,2,0:T(8,128)S(1)}, f32[16,256,64]{1,2,0:T(8,128)}, u32[]{:S(2)}) copy-start(f32[16,256,64]{1,2,0:T(8,128)} %get-tuple-element.256) | copy-start | bytes 3145732 | tf_op jit(solution)/shard_map/while/body/eval_jaxpr/cond
  493.9 7.5 %copy-start.5 = (bf16[512,16,64]{0,2,1:T(8,128)(2,1)S(1)}, bf16[512,16,64]{0,2,1:T(8,128)(2,1)}, u32[]{:S(2)}) copy-start(bf16[512,16,64]{0,2,1:T(8,128)(2,1)} %get-tuple-element.257) | copy-start | bytes 3145732 | tf_op jit(solution)/shard_map/while/body/eval_jaxpr/cond
  525.6 7.5 %copy-start.1 = (f32[16,256,64]{1,2,0:T(8,128)S(1)}, f32[16,256,64]{1,2,0:T(8,128)}, u32[]{:S(2)}) copy-start(f32[16,256,64]{1,2,0:T(8,128)} %get-tuple-element.256) | copy-start | bytes 3145732 | tf_op jit(solution)/shard_map/while/body/eval_jaxpr/cond
  525.6 7.5 %copy-start.5 = (bf16[512,16,64]{0,2,1:T(8,128)(2,1)S(1)}, bf16[512,16,64]{0,2,1:T(8,128)(2,1)}, u32[]{:S(2)}) copy-start(bf16[512,16,64]{0,2,1:T(8,128)(2,1)} %get-tuple-element.257) | copy-start | bytes 3145732 | tf_op jit(solution)/shard_map/while/body/eval_jaxpr/cond
  557.4 7.5 %copy-start.1 = (f32[16,256,64]{1,2,0:T(8,128)S(1)}, f32[16,256,64]{1,2,0:T(8,128)}, u32[]{:S(2)}) copy-start(f32[16,256,64]{1,2,0:T(8,128)} %get-tuple-element.256) | copy-start | bytes 3145732 | tf_op jit(solution)/shard_map/while/body/eval_jaxpr/cond
  557.4 7.5 %copy-start.5 = (bf16[512,16,64]{0,2,1:T(8,128)(2,1)S(1)}, bf16[512,16,64]{0,2,1:T(8,128)(2,1)}, u32[]{:S(2)}) copy-start(bf16[512,16,64]{0,2,1:T(8,128)(2,1)} %get-tuple-element.257) | copy-start | bytes 3145732 | tf_op jit(solution)/shard_map/while/body/eval_jaxpr/cond
  579.2 14.5 %collective-permute-start.1 = (bf16[256,1024]{1,0:T(8,128)(2,1)S(1)}, bf16[256,1024]{1,0:T(8,128)(2,1)S(1)}, u32[]{:S(2)}, u32[]{:S(2)}) collective-permute-start(bf16[256,1024]{1,0:T(8,128)(2,1)S(1)} %get-tuple-element.382), channel_id=1, source_target_pairs={{0,16},{1,17},{2,18},{3,19},{4,20},{5,21},{6,22},{7,23},{8,24},{9,... | collective-permute-start | bytes 1572872 | tf_op jit(solution)/shard_map/ppermute | solution.py:18
  (26 other events, 89.8 us)
Sparse Core Ops, SparseCore 0:
  109.2 153.5 all-gather.1
where the time goes:
time: 608 us; the launch traced here: 602 us
  waiting for transfers between devices  170 us (28%)
  local copies, waits for them, and re-layouts  167 us (27%)
  other arithmetic  115 us (19%)
  matrix products  85.1 us (14%)
  loops' own time  21.4 us (4%)
  blocking collectives  18 us (3%)
  between operations  13.6 us (2%)
  starting transfers between devices  11.5 us (2%)
    all_gather x1, waiting for transfers between devices, in_one_piece(): lax.all_gather(both, axis, axis=dim, tiled=True)  123 us
    dynamic_slice x16, local copies, waits for them, and re-layouts, one_block(): lax.dynamic_slice_in_dim(value_piece, offset, step_rows, 0)  42.7 us
    another operation x36, other arithmetic, one_block(): jnp.stack([updated[0][slot], updated[1][slot]])  39.4 us
    reduce_sum x12, other arithmetic, fold_block(): denominator = denominator * correction + jnp.sum(raised, axis=-1)  38.8 us
    dot_general x12, matrix products, fold_block(): jnp.einsum('hrk,khd->hrd', raised.astype(jnp.bfloat16), value_block, pref...  37.8 us
    dot_general x12, matrix products, fold_block(): jnp.einsum('rhd,khd->hrk', query_part, key_block, preferred_element_type=...  34.8 us
    ppermute x2, waiting for transfers between devices, from_partner(): return lax.ppermute(value, axis, pairs)  30.2 us
    squeeze x16, local copies, waits for them, and re-layouts, one_block(): part_state = tuple((member[part_index] for member in fold_state))  26.5 us
  transfers between devices with their start and end apart: 4, of which 4 were waited for; matrix products, arithmetic and copies ran while one was open for 2% of the time, Pallas kernels for 0%

commit v1 on v0

v1 whole, which is shorter than its diff:
```python
import functools
import math

import jax
import jax.numpy as jnp
from jax import lax
from jax.experimental import pallas as pl
from jax.experimental.pallas import tpu as pltpu
from jax.sharding import PartitionSpec as P

HEADS = 16
HEAD_DIM = 64
BLOCK_ROWS = 256
KEY_TILE = 512
UNROLL = 4
SUM_ROWS = 16
TO_LOG2 = math.log2(math.e) / math.sqrt(HEAD_DIM)
SCALE = 1.0 / math.sqrt(HEAD_DIM)
LEAST_TOTAL = 2.0**-90
MOST_TOTAL = 2.0**110
MIB = 1024 * 1024


def vmem():
    return pl.BlockSpec(memory_space=pltpu.VMEM)


def smem():
    return pl.BlockSpec(memory_space=pltpu.SMEM)


def query_kernel(x_ref, w_ref, len_ref, q_ref, starts_ref):
    rows, width = x_ref.shape
    lengths = len_ref[...].astype(jnp.float32).astype(jnp.bfloat16)
    lines, lanes = lengths.shape
    before = (
        lax.broadcasted_iota(jnp.int32, (lanes, lanes), 0)
        < lax.broadcasted_iota(jnp.int32, (lanes, lanes), 1)
    )
    within = jnp.dot(
        lengths, before.astype(jnp.float32).astype(jnp.bfloat16), preferred_element_type=jnp.float32
    )
    above = (
        lax.broadcasted_iota(jnp.int32, (lines, lines), 1)
        < lax.broadcasted_iota(jnp.int32, (lines, lines), 0)
    )
    column_sums = jnp.dot(
        above.astype(jnp.float32).astype(jnp.bfloat16), lengths, preferred_element_type=jnp.float32
    )
    starts_ref[...] = (within + jnp.sum(column_sums, axis=1, keepdims=True)).astype(jnp.int32)
    step = 256
    heads_step = step // HEAD_DIM
    for n in range(width // step):
        q = jnp.dot(
            x_ref[...], w_ref[:, n * step : (n + 1) * step], preferred_element_type=jnp.float32
        ).astype(jnp.bfloat16)
        qt = q.T
        for r in range(rows // BLOCK_ROWS):
            part = qt[:, r * BLOCK_ROWS : (r + 1) * BLOCK_ROWS]
            q_ref[r, n * heads_step : (n + 1) * heads_step] = part.reshape(
                heads_step, HEAD_DIM, BLOCK_ROWS
            )


def query_call(x, w_query, lengths):
    rows, width = x.shape
    copies = rows // BLOCK_ROWS
    return pl.pallas_call(
        query_kernel,
        out_shape=(
            jax.ShapeDtypeStruct((copies, HEADS, HEAD_DIM, BLOCK_ROWS), jnp.bfloat16),
            jax.ShapeDtypeStruct(lengths.shape, jnp.int32),
        ),
        in_specs=[vmem(), vmem(), vmem()],
        out_specs=(vmem(), vmem()),
        compiler_params=pltpu.CompilerParams(vmem_limit_bytes=16 * MIB),
        cost_estimate=pl.CostEstimate(
            flops=2 * rows * width * width, bytes_accessed=2 * (2 * rows * width + width * width),
            transcendentals=0,
        ),
        name="queries",
    )(x, w_query, lengths)


def norm_rows(values, gain):
    mean_square = jnp.mean(values * values, axis=-1, keepdims=True)
    return values * lax.rsqrt(mean_square + 1e-05) * gain.astype(jnp.float32)


def kv_kernel(x_ref, wd_ref, gain_ref, wk_ref, wv_ref, out_ref):
    blocks, groups, part, lanes = x_ref.shape
    rows = blocks * part
    width = wd_ref.shape[1]
    lhs = jnp.concatenate([x_ref[:, g].reshape(rows, lanes) for g in range(groups)], axis=1)
    projected = jnp.dot(lhs, wd_ref[...], preferred_element_type=jnp.float32)
    normed = norm_rows(projected, gain_ref[...]).astype(jnp.bfloat16)
    keys = jnp.dot(normed, wk_ref[...], preferred_element_type=jnp.float32)
    values = jnp.dot(normed, wv_ref[...], preferred_element_type=jnp.float32)
    copies = out_ref.shape[0]
    for h in range(width // HEAD_DIM):
        cut = slice(h * HEAD_DIM, (h + 1) * HEAD_DIM)
        both = jnp.concatenate([keys[:, cut], values[:, cut]], axis=1).astype(jnp.bfloat16)
        for r in range(copies):
            out_ref[r, h] = both


def kv_call(x, w_down, gain, w_key, w_value, copies):
    blocks, groups, part, lanes = x.shape
    rows = blocks * part
    width = w_down.shape[1]
    return pl.pallas_call(
        kv_kernel,
        out_shape=jax.ShapeDtypeStruct((copies, HEADS, rows, 2 * HEAD_DIM), jnp.bfloat16),
        in_specs=[vmem()] * 5,
        out_specs=vmem(),
        compiler_params=pltpu.CompilerParams(vmem_limit_bytes=32 * MIB),
        cost_estimate=pl.CostEstimate(
            flops=2 * rows * width * (groups * lanes + 2 * width),
            bytes_accessed=2 * (rows * groups * lanes + groups * lanes * width + 2 * width * width),
            transcendentals=0,
        ),
        name="keys_values",
    )(x, w_down, gain.reshape(1, -1), w_key, w_value)


def attend_kernel(
    group_ref, starts_s_ref, starts_ref, kv_ref, q_ref, out_ref,
    kvs, vt, qa, starts_b, acc, probs, flag,
):
    senders, blocks, part, lanes = kv_ref.shape
    row_blocks = q_ref.shape[0]
    patches = senders * blocks * part
    key_tiles = patches // KEY_TILE
    stride = q_ref.shape[2] * group_ref[1]
    group = group_ref[0]

    def first_row(m):
        return m * stride + group * BLOCK_ROWS

    for b in range(blocks):
        for s in range(senders):
            at = (b * senders + s) * part
            kvs[at : at + part, :] = kv_ref[s, b]
    for t in range(key_tiles):
        turned = kvs[t * KEY_TILE : (t + 1) * KEY_TILE, :].T
        vt[t, :HEAD_DIM, :] = turned[HEAD_DIM:, :]
        vt[t, HEAD_DIM:, :] = jnp.ones((SUM_ROWS, KEY_TILE), jnp.bfloat16)
    for line in range(patches // 128):
        row = jnp.broadcast_to(starts_ref[line : line + 1, :], (128, 128))
        starts_b[line * 128 : (line + 1) * 128, :] = row.T
    zeros = jnp.zeros((HEAD_DIM, BLOCK_ROWS), jnp.bfloat16)

    def prepare(m, carry):
        qa[m, :HEAD_DIM, :] = q_ref[m]
        qa[m, HEAD_DIM:, :] = zeros
        acc[m] = jnp.zeros(acc.shape[1:], jnp.float32)
        return carry

    lax.fori_loop(0, row_blocks, prepare, 0)
    qa[row_blocks] = jnp.zeros(qa.shape[1:], jnp.bfloat16)
    acc[row_blocks] = jnp.zeros(acc.shape[1:], jnp.float32)

    def ceil_blocks(rows):
        return jnp.minimum((jnp.maximum(rows, 0) + stride - 1) // stride, row_blocks)

    def lowest(kt):
        at = kt * KEY_TILE
        start = starts_s_ref[at // 128, 0]
        return ceil_blocks(start - group * BLOCK_ROWS - (BLOCK_ROWS - 1))

    def lowest_full(kt):
        at = kt * KEY_TILE + KEY_TILE - 1
        start = starts_s_ref[at // 128, 127]
        return ceil_blocks(start - group * BLOCK_ROWS)

    def weigh(kt, m, masked):
        keys = kvs[pl.ds(pl.multiple_of(kt * KEY_TILE, KEY_TILE), KEY_TILE), :]
        scores = jnp.dot(keys, qa[m], preferred_element_type=jnp.float32)
        p = jnp.exp2(scores * TO_LOG2)
        if masked:
            first = starts_b[pl.ds(pl.multiple_of(kt * KEY_TILE, KEY_TILE), KEY_TILE), :]
            first = jnp.concatenate([first] * (BLOCK_ROWS // 128), axis=1)
            rows = first_row(m) + lax.broadcasted_iota(jnp.int32, (KEY_TILE, BLOCK_ROWS), 1)
            p = jnp.where(first <= rows, p, 0.0)
        return p.astype(jnp.bfloat16)

    def fold(kt, m, p):
        acc[m] = acc[m] + jnp.dot(vt[kt], p, preferred_element_type=jnp.float32)

    def run(masked, first_of, past_of):
        total = jnp.int32(0)
        for kt in range(key_tiles):
            total = total + jnp.maximum(past_of(kt) - first_of(kt), 0)

        def settle(kt, m):
            def more(state):
                kt, m = state
                return jnp.logical_and(kt < key_tiles, m >= past_of(jnp.minimum(kt, key_tiles - 1)))

            def on(state):
                kt, _ = state
                return kt + 1, first_of(jnp.minimum(kt + 1, key_tiles - 1))

            return lax.while_loop(more, on, (kt, m))

        def advance(kt, m):
            return settle(kt, m + 1)

        def usable(kt, m):
            valid = kt < key_tiles
            return jnp.where(valid, kt, 0), jnp.where(valid, m, row_blocks)

        steps = (total + UNROLL - 1) // UNROLL
        start = settle(jnp.int32(0), first_of(0))

        def take(state):
            pairs = []
            for _ in range(UNROLL):
                pairs.append(usable(*state))
                state = advance(*state)
            return pairs, state

        @pl.when(total > 0)
        def _():
            pairs, state = take(start)
            for i, (kt, m) in enumerate(pairs):
                probs[i] = weigh(kt, m, masked)

            def body(_, carry):
                state, flat = carry
                old = [(flat[2 * i], flat[2 * i + 1]) for i in range(UNROLL)]
                pairs, state = take(state)
                for i in range(UNROLL):
                    ready = probs[i]
                    fold(*old[i], ready)
                    probs[i] = weigh(*pairs[i], masked)
                return state, tuple(v for pair in pairs for v in pair)

            flat = tuple(v for pair in pairs for v in pair)
            _, flat = lax.fori_loop(0, steps - 1, body, (state, flat))
            for i in range(UNROLL):
                fold(flat[2 * i], flat[2 * i + 1], probs[i])

    run(False, lowest_full, lambda kt: jnp.int32(row_blocks))
    run(True, lowest, lowest_full)

    def finish(m, worst):
        totals = acc[m, HEAD_DIM : HEAD_DIM + 1, :]
        out_ref[m] = (acc[m, :HEAD_DIM, :] * (1.0 / totals)).astype(jnp.bfloat16)
        fine = jnp.logical_and(totals > LEAST_TOTAL, totals < MOST_TOTAL)
        return jnp.maximum(worst, jnp.where(fine, 0.0, 1.0))

    worst = lax.fori_loop(0, row_blocks, finish, jnp.zeros((1, BLOCK_ROWS), jnp.float32))
    flag[0] = jnp.max(worst)

    @pl.when(flag[0] > 0.0)
    def _():
        def redo(m, carry):
            rows = first_row(m) + lax.broadcasted_iota(jnp.int32, (KEY_TILE, BLOCK_ROWS), 1)

            def masked_scores(kt):
                at = pl.ds(pl.multiple_of(kt * KEY_TILE, KEY_TILE), KEY_TILE)
                scores = jnp.dot(kvs[at, :], qa[m], preferred_element_type=jnp.float32) * SCALE
                first = jnp.concatenate([starts_b[at, :]] * (BLOCK_ROWS // 128), axis=1)
                return scores, first <= rows

            def fold_max(kt, peak):
                scores, allowed = masked_scores(kt)
                masked = jnp.where(allowed, scores, -3e38)
                return jnp.maximum(peak, jnp.max(masked, axis=0, keepdims=True))

            peak = lax.fori_loop(
                0, key_tiles, fold_max, jnp.full((1, BLOCK_ROWS), -3e38, jnp.float32)
            )
            acc[m] = jnp.zeros(acc.shape[1:], jnp.float32)

            def fold_sum(kt, inner):
                scores, allowed = masked_scores(kt)
                p = jnp.where(allowed, jnp.exp(jnp.where(allowed, scores - peak, 0.0)), 0.0)
                fold(kt, m, p.astype(jnp.bfloat16))
                return inner

            lax.fori_loop(0, key_tiles, fold_sum, 0)
            totals = acc[m, HEAD_DIM : HEAD_DIM + 1, :]
            out_ref[m] = (acc[m, :HEAD_DIM, :] * (1.0 / totals)).astype(jnp.bfloat16)
            return carry

        lax.fori_loop(0, row_blocks, redo, 0)


def attend_call(group, starts, kv, q):
    senders, blocks, part, lanes = kv.shape
    row_blocks = q.shape[0]
    patches = senders * blocks * part
    key_tiles = patches // KEY_TILE
    return pl.pallas_call(
        attend_kernel,
        out_shape=jax.ShapeDtypeStruct(q.shape, jnp.bfloat16),
        in_specs=[smem(), smem(), vmem(), vmem(), vmem()],
        out_specs=vmem(),
        scratch_shapes=[
            pltpu.VMEM((patches, lanes), jnp.bfloat16),
            pltpu.VMEM((key_tiles, HEAD_DIM + SUM_ROWS, KEY_TILE), jnp.bfloat16),
            pltpu.VMEM((row_blocks + 1, 2 * HEAD_DIM, BLOCK_ROWS), jnp.bfloat16),
            pltpu.VMEM((patches, 128), jnp.int32),
            pltpu.VMEM((row_blocks + 1, HEAD_DIM + SUM_ROWS, BLOCK_ROWS), jnp.float32),
            pltpu.VMEM((UNROLL, KEY_TILE, BLOCK_ROWS), jnp.bfloat16),
            pltpu.SMEM((1,), jnp.float32),
        ],
        compiler_params=pltpu.CompilerParams(vmem_limit_bytes=32 * MIB),
        cost_estimate=pl.CostEstimate(
            flops=2 * patches * row_blocks * BLOCK_ROWS * 2 * HEAD_DIM,
            bytes_accessed=2 * (kv.size + 2 * q.size),
            transcendentals=patches * row_blocks * BLOCK_ROWS // 2,
        ),
        name="attend",
    )(group, starts, starts, kv, q)


def out_kernel(h_ref, w_ref, x_ref, gain_ref, out_ref):
    copies = h_ref.shape[0]
    width = w_ref.shape[0]
    for r in range(copies):
        cut = slice(r * BLOCK_ROWS, (r + 1) * BLOCK_ROWS)
        head_out = h_ref[r].reshape(width, BLOCK_ROWS).T
        residual = x_ref[cut, :].astype(jnp.float32) + jnp.dot(
            head_out, w_ref[...], preferred_element_type=jnp.float32
        )
        out_ref[cut, :] = norm_rows(residual, gain_ref[...]).astype(jnp.bfloat16)


def out_call(head_out, w_out, x, gain):
    rows, width = x.shape
    return pl.pallas_call(
        out_kernel,
        out_shape=jax.ShapeDtypeStruct(x.shape, jnp.bfloat16),
        in_specs=[vmem()] * 4,
        out_specs=vmem(),
        compiler_params=pltpu.CompilerParams(vmem_limit_bytes=16 * MIB),
        cost_estimate=pl.CostEstimate(
            flops=2 * rows * width * width, bytes_accessed=2 * (3 * rows * width + width * width),
            transcendentals=rows,
        ),
        name="outputs",
    )(head_out, w_out, x, gain.reshape(1, -1))


def per_device(
    byte_states, patch_latents, patch_lengths, w_down, kv_gain, w_query, w_key, w_value, w_out,
    out_gain,
):
    seqs, mps = lax.axis_size("seq"), lax.axis_size("mp")
    copies = mps // HEADS
    x = byte_states[0]
    patches_here, features = patch_latents.shape[1:]
    part = patches_here // mps

    sent = patch_latents.reshape(seqs * mps, part, features)
    latents = lax.all_to_all(sent, ("seq", "mp"), 0, 0, tiled=True)
    latents = latents.reshape(seqs, mps, part, features)
    lengths = patch_lengths[0].reshape(-1, 128)
    queries, starts = query_call(x, w_query, lengths)
    queries = queries.reshape(mps, HEAD_DIM, BLOCK_ROWS)
    queries = lax.all_to_all(queries, "mp", 0, 0, tiled=True)

    kv = kv_call(latents, w_down, kv_gain, w_key, w_value, copies)
    kv = lax.all_to_all(kv.reshape(mps, seqs * part, 2 * HEAD_DIM), "mp", 0, 0, tiled=True)
    kv = kv.reshape(mps, seqs, part, 2 * HEAD_DIM)

    group = jnp.stack([lax.axis_index("mp") // HEADS, jnp.int32(copies)])
    head_out = attend_call(group, starts, kv, queries)
    head_out = lax.all_to_all(head_out, "mp", 0, 0, tiled=True)
    decoded = out_call(
        head_out.reshape(copies, HEADS, HEAD_DIM, BLOCK_ROWS), w_out, x, out_gain
    )
    return decoded[None]


def solution(mesh):
    return jax.shard_map(
        per_device,
        mesh=mesh,
        in_specs=(
            P("seq", "mp", None),
            P(None, "seq", "mp"),
            P("seq", None),
            P(),
            P(),
            P(),
            P(),
            P(),
            P(),
            P(),
        ),
        out_specs=P("seq", "mp", None),
        check_vma=False,
    )
```

time: 608 us -> 296 us (0.49)
  Pallas kernels: 0 us -> 203 us
  local copies, waits for them, and re-layouts: 167 us -> 11 us
  waiting for transfers between devices: 170 us -> 54.3 us
  other arithmetic: 115 us -> 0.08 us
  matrix products: 85.1 us -> 0 us
  loops' own time: 21.4 us -> 0 us
  blocking collectives: 18 us -> 0 us
  starting transfers between devices: 11.5 us -> 26.5 us
  between operations: 13.6 us -> 0.15 us
    pallas_call x0 -> x4, Pallas kernels: none -> 203 us  [the longest x1 196 us: attend_call(): pl.pallas_call(attend_kernel, out_shape=jax.ShapeDtypeStruct(q.shape, jnp...]
    all_gather x1 -> x0, waiting for transfers between devices: 123 us -> none  [in_one_piece(): lax.all_gather(both, axis, axis=dim, tiled=True)]
    dot_general x29 -> x0, matrix products: 85.1 us -> none  [the longest x12 37.8 us: fold_block(): jnp.einsum('hrk,khd->hrd', raised.astype(jnp.bfloat16), value_block, pref...]
    dynamic_slice x32 -> x0, local copies, waits for them, and re-layouts: 55.3 us -> none  [the longest x16 42.7 us: one_block(): lax.dynamic_slice_in_dim(value_piece, offset, step_rows, 0)]
    another operation x38 -> x1, other arithmetic: 39.7 us -> 0.08 us  [per_device(): group = jnp.stack([lax.axis_index('mp') // HEADS, jnp.int32(copies)])]
    reduce_sum x12 -> x0, other arithmetic: 38.8 us -> none  [fold_block(): denominator = denominator * correction + jnp.sum(raised, axis=-1)]
    all_to_all x1 -> x4, waiting for transfers between devices: 16.8 us -> 54.3 us  [the longest x1 16.3 us: per_device(): lax.all_to_all(kv.reshape(mps, seqs * part, 2 * HEAD_DIM), 'mp', 0, 0, ti...]
    ppermute x2 -> x0, waiting for transfers between devices: 30.2 us -> none  [from_partner(): return lax.ppermute(value, axis, pairs)]
  transfers between devices with their start and end apart: 4 -> 4, of which waited for: 4 -> 4; matrix products, arithmetic and copies ran while one was open for 2% -> 0% of each run, Pallas kernels for 0% -> 2%
where the time goes in v1:
time: 296 us; the launch traced here: 295 us
  Pallas kernels  203 us (69%)
  waiting for transfers between devices  54.3 us (18%)
  starting transfers between devices  26.5 us (9%)
  local copies, waits for them, and re-layouts  11 us (4%)
    pallas_call x1, Pallas kernels, attend_call(): pl.pallas_call(attend_kernel, out_shape=jax.ShapeDtypeStruct(q.shape, jnp...  196 us
    all_to_all x1, waiting for transfers between devices, per_device(): lax.all_to_all(kv.reshape(mps, seqs * part, 2 * HEAD_DIM), 'mp', 0, 0, ti...  16.3 us
    all_to_all x1, waiting for transfers between devices, per_device(): head_out = lax.all_to_all(head_out, 'mp', 0, 0, tiled=True)  15.4 us
    all_to_all x1, waiting for transfers between devices, per_device(): latents = lax.all_to_all(sent, ('seq', 'mp'), 0, 0, tiled=True)  13 us
    unnamed x24, local copies, waits for them, and re-layouts  11 us
    all_to_all x1, starting transfers between devices, per_device(): latents = lax.all_to_all(sent, ('seq', 'mp'), 0, 0, tiled=True)  10.3 us
    all_to_all x1, waiting for transfers between devices, per_device(): queries = lax.all_to_all(queries, 'mp', 0, 0, tiled=True)  9.56 us
  transfers between devices with their start and end apart: 4, of which 4 were waited for; matrix products, arithmetic and copies ran while one was open for 0% of the time, Pallas kernels for 2%

profile of v1, /device:TPU:24, one launch (start us, length us, event | category | flops | bytes accessed | tf_op | source)
XLA Modules:
  0.0 295.0 jit_solution(5406838003123075828)
XLA Ops:
  0.0 10.3 %all-to-all-start = ((bf16[128,32,128]{2,1,0:T(8,128)(2,1)}), bf16[128,32,128]{2,1,0:T(8,128)(2,1)S(1)}, u32[]{:S(2)}, u32[]{:S(2)}) async-start(bf16[128,32,128]{2,1,0:T(8,128)(2,1)} %bitcast.17), calls=%async_computation | async-start | bytes 2097152 | tf_op jit(solution)/shard_map/all_to_all | solution.py:359
  10.3 0.0 copy-start.6
  10.3 1.2 copy-done.6
  11.5 1.6 copy-done.8
  13.1 1.3 queries.1
  14.5 1.0 copy-done.4
  15.4 13.0 %all-to-all-done = bf16[128,32,128]{2,1,0:T(8,128)(2,1)S(1)} async-done(((bf16[128,32,128]{2,1,0:T(8,128)(2,1)}), bf16[128,32,128]{2,1,0:T(8,128)(2,1)S(1)}, u32[]{:S(2)}, u32[]{:S(2)}) %all-to-all-start) | async-done | bytes 1048608 | tf_op jit(solution)/shard_map/all_to_all | solution.py:359
  28.4 5.7 %all-to-all-start.2 = ((bf16[32,64,256]{2,1,0:T(8,128)(2,1)}), bf16[32,64,256]{2,1,0:T(8,128)(2,1)}, u32[]{:S(2)}, u32[]{:S(2)}) async-start(bf16[32,64,256]{2,1,0:T(8,128)(2,1)} %bitcast.13), calls=%async_computation.2 | async-start | bytes 2097152 | tf_op jit(solution)/shard_map/all_to_all | solution.py:364
  34.2 0.0 copy-done.10
  34.2 0.0 copy-start
  34.2 3.4 %copy-done = bf16[4096,1024]{1,0:T(8,128)(2,1)S(1)} copy-done((bf16[4096,1024]{1,0:T(8,128)(2,1)S(1)}, bf16[4096,1024]{1,0:T(8,128)(2,1)}, u32[]{:S(2)}) %copy-start) | copy-done | bytes 8388632
  37.6 1.6 copy-done.3
  39.2 3.2 %keys_values.1 = bf16[2,16,128,128]{3,2,1,0:T(8,128)(2,1)} custom-call(bf16[4,32,32,128]{3,2,1,0:T(8,128)(2,1)S(1)} %bitcast.11, bf16[4096,1024]{1,0:T(8,128)(2,1)S(1)} %copy-done, bf16[1,1024]{1,0:T(2,128)(2,1)S(1)} %reshape.26.gain_ref, bf16[1024,1024]{1,0:T(8,128)(2,1)S(1)} %copy-done.2, bf16[1024,1024]{1,0:T(8,128)(2,1)S(1)} %copy-done.3), custom_call_target="tpu_custom_call" | custom-call | flops 1610612736 | bytes 13631488 | tf_op jit(solution)/shard_map/keys_values/pallas_call | solution.py:111
  42.3 9.6 %all-to-all-done.2.q_ref = bf16[32,64,256]{2,1,0:T(8,128)(2,1)} async-done(((bf16[32,64,256]{2,1,0:T(8,128)(2,1)}), bf16[32,64,256]{2,1,0:T(8,128)(2,1)}, u32[]{:S(2)}, u32[]{:S(2)}) %all-to-all-start.2) | async-done | bytes 1048608 | tf_op jit(solution)/shard_map/all_to_all | solution.py:364
  51.9 5.2 %all-to-all-start.1 = ((bf16[32,128,128]{2,1,0:T(8,128)(2,1)}), bf16[32,128,128]{2,1,0:T(8,128)(2,1)S(1)}, u32[]{:S(2)}, u32[]{:S(2)}) async-start(bf16[32,128,128]{2,1,0:T(8,128)(2,1)} %bitcast.5), calls=%async_computation.1 | async-start | bytes 2097152 | tf_op jit(solution)/shard_map/all_to_all | solution.py:367
  57.1 0.1 pad_add_fusion.group_ref
  57.2 16.3 %all-to-all-done.1 = bf16[32,128,128]{2,1,0:T(8,128)(2,1)S(1)} async-done(((bf16[32,128,128]{2,1,0:T(8,128)(2,1)}), bf16[32,128,128]{2,1,0:T(8,128)(2,1)S(1)}, u32[]{:S(2)}, u32[]{:S(2)}) %all-to-all-start.1) | async-done | bytes 1048608 | tf_op jit(solution)/shard_map/all_to_all | solution.py:367
  73.5 196.1 %attend.1 = bf16[32,64,256]{2,1,0:T(8,128)(2,1)S(1)} custom-call(s32[2]{0:T(128)S(1)} %pad_add_fusion.group_ref, s32[32,128]{1,0:T(8,128)S(1)} %get-tuple-element.7.starts_s_ref.starts_ref, s32[32,128]{1,0:T(8,128)S(1)} %get-tuple-element.7.starts_s_ref.starts_ref, bf16[32,4,32,128]{3,2,1,0:T(8,128)(2,1)S(1)} %bitcast.12, ...), custom_call_target="tpu_custom_call" | custom-call | flops 8589934592 | bytes 3145728 | tf_op jit(solution)/shard_map/attend/pallas_call | solution.py:296
  269.6 0.0 copy-start.5
  269.6 1.0 copy-done.5
  270.5 5.3 %all-to-all-start.3 = ((bf16[32,64,256]{2,1,0:T(8,128)(2,1)}), bf16[32,64,256]{2,1,0:T(8,128)(2,1)S(1)}, u32[]{:S(2)}, u32[]{:S(2)}) async-start(bf16[32,64,256]{2,1,0:T(8,128)(2,1)} %copy-done.5), calls=%async_computation.3 | async-start | bytes 2097152 | tf_op jit(solution)/shard_map/all_to_all | solution.py:372
  275.9 15.4 %all-to-all-done.3 = bf16[32,64,256]{2,1,0:T(8,128)(2,1)S(1)} async-done(((bf16[32,64,256]{2,1,0:T(8,128)(2,1)}), bf16[32,64,256]{2,1,0:T(8,128)(2,1)S(1)}, u32[]{:S(2)}, u32[]{:S(2)}) %all-to-all-start.3) | async-done | bytes 1048608 | tf_op jit(solution)/shard_map/all_to_all | solution.py:372
  291.3 1.2 copy-done.7
  292.6 2.4 outputs.1
  (15 shorter events, 0.0 us)
Async XLA Ops:
  0.0 10.3 %copy-start.9 = (s32[1,4096]{1,0:T(1,128)S(1)}, s32[1,4096]{1,0:T(1,128)}, u32[]{:S(2)}) copy-start(s32[1,4096]{1,0:T(1,128)} %param.12) | copy-start | bytes 49156
  0.0 28.4 %all-to-all-start = ((bf16[128,32,128]{2,1,0:T(8,128)(2,1)}), bf16[128,32,128]{2,1,0:T(8,128)(2,1)S(1)}, u32[]{:S(2)}, u32[]{:S(2)}) async-start(bf16[128,32,128]{2,1,0:T(8,128)(2,1)} %bitcast.17), calls=%async_computation | async-start | bytes 2097152 | tf_op jit(solution)/shard_map/all_to_all | solution.py:359
  10.3 1.2 copy-start.6
  11.5 1.6 copy-start.8
  13.1 21.1 %copy-start.10 = (bf16[1024]{0:T(1024)(128)(2,1)S(1)}, bf16[1024]{0:T(1024)(128)(2,1)}, u32[]{:S(2)}) copy-start(bf16[1024]{0:T(1024)(128)(2,1)} %param.14) | copy-start | bytes 6148
  13.1 21.1 %copy-start.2 = (bf16[1024,1024]{1,0:T(8,128)(2,1)S(1)}, bf16[1024,1024]{1,0:T(8,128)(2,1)}, u32[]{:S(2)}) copy-start(bf16[1024,1024]{1,0:T(8,128)(2,1)} %wk_ref.1) | copy-start | bytes 6291460
  14.5 1.0 copy-start.4
  28.4 23.5 %all-to-all-start.2 = ((bf16[32,64,256]{2,1,0:T(8,128)(2,1)}), bf16[32,64,256]{2,1,0:T(8,128)(2,1)}, u32[]{:S(2)}, u32[]{:S(2)}) async-start(bf16[32,64,256]{2,1,0:T(8,128)(2,1)} %bitcast.13), calls=%async_computation.2 | async-start | bytes 2097152 | tf_op jit(solution)/shard_map/all_to_all | solution.py:364
  34.2 3.4 %copy-start = (bf16[4096,1024]{1,0:T(8,128)(2,1)S(1)}, bf16[4096,1024]{1,0:T(8,128)(2,1)}, u32[]{:S(2)}) copy-start(bf16[4096,1024]{1,0:T(8,128)(2,1)} %wd_ref.1) | copy-start | bytes 25165828
  37.6 1.6 copy-start.3
  51.9 21.6 %all-to-all-start.1 = ((bf16[32,128,128]{2,1,0:T(8,128)(2,1)}), bf16[32,128,128]{2,1,0:T(8,128)(2,1)S(1)}, u32[]{:S(2)}, u32[]{:S(2)}) async-start(bf16[32,128,128]{2,1,0:T(8,128)(2,1)} %bitcast.5), calls=%async_computation.1 | async-start | bytes 2097152 | tf_op jit(solution)/shard_map/all_to_all | solution.py:367
  73.5 202.4 %copy-start.11 = (bf16[1024]{0:T(1024)(128)(2,1)S(1)}, bf16[1024]{0:T(1024)(128)(2,1)}, u32[]{:S(2)}) copy-start(bf16[1024]{0:T(1024)(128)(2,1)} %param.19) | copy-start | bytes 6148
  269.6 1.0 copy-start.5
  270.5 20.8 %copy-start.1 = (bf16[1024,1024]{1,0:T(8,128)(2,1)S(1)}, bf16[1024,1024]{1,0:T(8,128)(2,1)}, u32[]{:S(2)}) copy-start(bf16[1024,1024]{1,0:T(8,128)(2,1)} %w_ref.3) | copy-start | bytes 6291460
  270.5 20.8 %all-to-all-start.3 = ((bf16[32,64,256]{2,1,0:T(8,128)(2,1)}), bf16[32,64,256]{2,1,0:T(8,128)(2,1)S(1)}, u32[]{:S(2)}, u32[]{:S(2)}) async-start(bf16[32,64,256]{2,1,0:T(8,128)(2,1)} %copy-done.5), calls=%async_computation.3 | async-start | bytes 2097152 | tf_op jit(solution)/shard_map/all_to_all | solution.py:372
  291.3 1.2 copy-start.7

commit v2 on v1

v2 whole, which is shorter than its diff:
```python
import functools
import math

import jax
import jax.numpy as jnp
from jax import lax
from jax.experimental import pallas as pl
from jax.experimental.pallas import tpu as pltpu
from jax.sharding import PartitionSpec as P

HEADS = 16
HEAD_DIM = 64
BLOCK_ROWS = 256
KEY_TILE = 512
UNROLL = 8
SUM_ROWS = 16
TO_LOG2 = math.log2(math.e) / math.sqrt(HEAD_DIM)
SCALE = 1.0 / math.sqrt(HEAD_DIM)
LEAST_TOTAL = 2.0**-90
MOST_TOTAL = 2.0**110
MIB = 1024 * 1024


def vmem():
    return pl.BlockSpec(memory_space=pltpu.VMEM)


def smem():
    return pl.BlockSpec(memory_space=pltpu.SMEM)


def hbm():
    return pl.BlockSpec(memory_space=pltpu.HBM)


def ones_where(mask):
    return mask.astype(jnp.float32).astype(jnp.bfloat16)


def iota(shape, dim):
    return lax.broadcasted_iota(jnp.int32, shape, dim)


def exact_dot(a, b):
    return jnp.dot(a, b, preferred_element_type=jnp.float32)


def patch_tables(lengths, starts_ref, counts_ref):
    lines, lanes = lengths.shape
    values = lengths.astype(jnp.float32).astype(jnp.bfloat16)
    square = (lanes, lanes)
    within = exact_dot(values, ones_where(iota(square, 0) < iota(square, 1)))
    small = (lines, lines)
    above = exact_dot(ones_where(iota(small, 1) < iota(small, 0)), values)
    starts = (within + jnp.sum(above, axis=1, keepdims=True)).astype(jnp.int32)
    starts_ref[...] = starts
    spots = counts_ref.shape[0]
    tops, lows = [], []
    for line in range(lines):
        row = starts[line : line + 1, :]
        tops.append(ones_where(iota((spots, lanes), 0) == lax.shift_right_logical(row, 7)))
        lows.append(ones_where(iota((128, lanes), 0) == jnp.bitwise_and(row, 127)))
    present = lax.dot_general(
        jnp.concatenate(tops, axis=1),
        jnp.concatenate(lows, axis=1),
        (((1,), (1,)), ((), ())),
        preferred_element_type=jnp.float32,
    ).astype(jnp.bfloat16)
    along = exact_dot(present, ones_where(iota((128, 128), 0) <= iota((128, 128), 1)))
    before = exact_dot(ones_where(iota((spots, spots), 1) < iota((spots, spots), 0)), present)
    counts_ref[...] = (along + jnp.sum(before, axis=1, keepdims=True)).astype(jnp.int32)


def query_kernel(x_ref, w_ref, len_ref, buf_ref, starts_ref, counts_ref, staged, sems):
    rows, width = x_ref.shape
    step = 256
    heads_step = step // HEAD_DIM
    copies = rows // BLOCK_ROWS
    half = BLOCK_ROWS // 128
    sent = []
    for n in range(width // step):
        q = jnp.dot(
            x_ref[...], w_ref[:, n * step : (n + 1) * step], preferred_element_type=jnp.float32
        ).astype(jnp.bfloat16)
        qt = q.T
        for r in range(copies):
            for h in range(heads_step):
                for b in range(half):
                    at = r * BLOCK_ROWS + b * 128
                    staged[r, n * heads_step + h, b * HEAD_DIM : (b + 1) * HEAD_DIM, :] = qt[
                        h * HEAD_DIM : (h + 1) * HEAD_DIM, at : at + 128
                    ]
            cut = pl.ds(n * heads_step, heads_step)
            send = pltpu.make_async_copy(
                staged.at[r, cut],
                buf_ref.at[pl.ds(r * HEADS + n * heads_step, heads_step), pl.ds(128, 128)],
                sems.at[n * copies + r],
            )
            send.start()
            sent.append(send)
    patch_tables(len_ref[...], starts_ref, counts_ref)
    for send in sent:
        send.wait()


def query_call(x, w_query, lengths, seq_len):
    rows, width = x.shape
    copies = rows // BLOCK_ROWS
    return pl.pallas_call(
        query_kernel,
        out_shape=(
            jax.ShapeDtypeStruct((copies * HEADS, 256, 128), jnp.bfloat16),
            jax.ShapeDtypeStruct(lengths.shape, jnp.int32),
            jax.ShapeDtypeStruct((seq_len // 128, 128), jnp.int32),
        ),
        in_specs=[vmem(), vmem(), vmem()],
        out_specs=(hbm(), vmem(), vmem()),
        scratch_shapes=[
            pltpu.VMEM((copies, HEADS, 128, 128), jnp.bfloat16),
            pltpu.SemaphoreType.DMA((copies * width // 256,)),
        ],
        compiler_params=pltpu.CompilerParams(vmem_limit_bytes=16 * MIB),
        cost_estimate=pl.CostEstimate(
            flops=2 * rows * width * width, bytes_accessed=2 * (2 * rows * width + width * width),
            transcendentals=0,
        ),
        name="queries",
    )(x, w_query, lengths)


def norm_rows(values, gain):
    mean_square = jnp.mean(values * values, axis=-1, keepdims=True)
    return values * lax.rsqrt(mean_square + 1e-05) * gain.astype(jnp.float32)


WD_PARTS = 8


def kv_kernel(
    x_ref, wd_ref, gain_ref, wk_ref, wv_ref, old_ref, buf_ref, wd, wk, wv, acc, staged, sems, outs
):
    blocks, groups, part, lanes = x_ref.shape
    rows = blocks * part
    depth = wd_ref.shape[0] // WD_PARTS
    per_part = groups // WD_PARTS
    loads = [
        pltpu.make_async_copy(
            wd_ref.at[pl.ds(i * depth, depth)], wd.at[pl.ds(i * depth, depth)], sems.at[i]
        )
        for i in range(WD_PARTS)
    ]
    loads.append(pltpu.make_async_copy(wk_ref, wk, sems.at[WD_PARTS]))
    loads.append(pltpu.make_async_copy(wv_ref, wv, sems.at[WD_PARTS + 1]))
    for load in loads:
        load.start()
    for i in range(WD_PARTS):
        lhs = jnp.concatenate(
            [x_ref[:, i * per_part + g].reshape(rows, lanes) for g in range(per_part)], axis=1
        )
        loads[i].wait()
        product = jnp.dot(
            lhs, wd[i * depth : (i + 1) * depth, :], preferred_element_type=jnp.float32
        )
        acc[...] = product if i == 0 else acc[...] + product
    normed = norm_rows(acc[...], gain_ref[...]).astype(jnp.bfloat16)
    loads[WD_PARTS].wait()
    loads[WD_PARTS + 1].wait()
    copies = buf_ref.shape[0] // HEADS
    step = 256
    heads_step = step // HEAD_DIM
    sent = []
    for n in range(wk.shape[1] // step):
        cut = slice(n * step, (n + 1) * step)
        keys = jnp.dot(normed, wk[:, cut], preferred_element_type=jnp.float32)
        values = jnp.dot(normed, wv[:, cut], preferred_element_type=jnp.float32)
        for h in range(heads_step):
            own = slice(h * HEAD_DIM, (h + 1) * HEAD_DIM)
            staged[n * heads_step + h] = jnp.concatenate(
                [keys[:, own], values[:, own]], axis=1
            ).astype(jnp.bfloat16)
        for r in range(copies):
            send = pltpu.make_async_copy(
                staged.at[pl.ds(n * heads_step, heads_step)],
                buf_ref.at[pl.ds(r * HEADS + n * heads_step, heads_step), pl.ds(0, 128)],
                outs.at[n * copies + r],
            )
            send.start()
            sent.append(send)
    for send in sent:
        send.wait()


def kv_call(x, w_down, gain, w_key, w_value, buf):
    blocks, groups, part, lanes = x.shape
    rows = blocks * part
    width = w_down.shape[1]
    return pl.pallas_call(
        kv_kernel,
        out_shape=jax.ShapeDtypeStruct(buf.shape, buf.dtype),
        in_specs=[vmem(), hbm(), vmem(), hbm(), hbm(), hbm()],
        out_specs=hbm(),
        input_output_aliases={5: 0},
        scratch_shapes=[
            pltpu.VMEM(w_down.shape, jnp.bfloat16),
            pltpu.VMEM(w_key.shape, jnp.bfloat16),
            pltpu.VMEM(w_value.shape, jnp.bfloat16),
            pltpu.VMEM((rows, width), jnp.float32),
            pltpu.VMEM((HEADS, rows, 2 * HEAD_DIM), jnp.bfloat16),
            pltpu.SemaphoreType.DMA((WD_PARTS + 2,)),
            pltpu.SemaphoreType.DMA((buf.shape[0] // HEADS * width // 256,)),
        ],
        compiler_params=pltpu.CompilerParams(vmem_limit_bytes=50 * MIB),
        cost_estimate=pl.CostEstimate(
            flops=2 * rows * width * (groups * lanes + 2 * width),
            bytes_accessed=2 * (rows * groups * lanes + groups * lanes * width + 2 * width * width),
            transcendentals=0,
        ),
        name="keys_values",
    )(x, w_down, gain.reshape(1, -1), w_key, w_value, buf)


def attend_kernel(
    blocks, group_ref, starts_ref, counts_ref, in_ref, out_ref,
    kvs, vt, order, acc, probs, staged, lows, flag, sems,
):
    row_blocks = in_ref.shape[0]
    senders = row_blocks
    part = 128 // blocks
    patches = kvs.shape[0]
    key_tiles = patches // KEY_TILE
    stride = BLOCK_ROWS * group_ref[1]
    group = group_ref[0]

    def ceil_blocks(rows):
        return jnp.minimum((jnp.maximum(rows, 0) + stride - 1) // stride, row_blocks)

    total = jnp.int32(0)
    for kt in range(lows.shape[0]):
        if kt < key_tiles:
            start = starts_ref[kt * KEY_TILE // 128, 0]
            low = ceil_blocks(start - group * BLOCK_ROWS - (BLOCK_ROWS - 1))
            total = total + row_blocks - low
        else:
            low = jnp.int32(row_blocks)
        lows[kt] = low

    for b in range(blocks):
        for s in range(senders):
            at = (b * senders + s) * part
            kvs[at : at + part, :] = in_ref[s, b * part : (b + 1) * part, :]
    for t in range(key_tiles):
        turned = kvs[t * KEY_TILE : (t + 1) * KEY_TILE, :].T
        vt[t, :HEAD_DIM, :] = turned[HEAD_DIM:, :]
        vt[t, HEAD_DIM:, :] = jnp.ones((SUM_ROWS, KEY_TILE), jnp.bfloat16)
    order[...] = iota(order.shape, 0)

    def clear(m, carry):
        acc[m] = jnp.zeros(acc.shape[1:], jnp.float32)
        return carry

    lax.fori_loop(0, row_blocks + 1, clear, 0)
    zeros = jnp.zeros((HEAD_DIM, BLOCK_ROWS), jnp.bfloat16)
    lanes = BLOCK_ROWS // 128

    def query_rows(m):
        halves = [
            in_ref[m, 128 + b * HEAD_DIM : 128 + (b + 1) * HEAD_DIM, :] for b in range(lanes)
        ]
        return jnp.concatenate([jnp.concatenate(halves, axis=1), zeros], axis=0)

    def allowed_keys(m, kt):
        line = (m * stride + group * BLOCK_ROWS) // 128
        met = [counts_ref[pl.ds(line + b, 1), :] for b in range(lanes)]
        here = jnp.concatenate(met, axis=1) - kt * KEY_TILE
        return jnp.concatenate([order[...]] * lanes, axis=1) < here

    def key_rows(kt):
        return kvs[pl.ds(pl.multiple_of(kt * KEY_TILE, KEY_TILE), KEY_TILE), :]

    def weigh(kt, m):
        kt, m = jnp.minimum(kt, key_tiles - 1), jnp.minimum(m, row_blocks - 1)
        scores = jnp.dot(key_rows(kt), query_rows(m), preferred_element_type=jnp.float32)
        p = jnp.where(allowed_keys(m, kt), jnp.exp2(scores * TO_LOG2), 0.0)
        return p.astype(jnp.bfloat16)

    def fold(kt, m, p):
        kt = jnp.minimum(kt, key_tiles - 1)
        acc[m] = acc[m] + jnp.dot(vt[kt], p, preferred_element_type=jnp.float32)

    def advance(kt, m):
        wrap = m + 1 >= row_blocks
        kt = kt + wrap.astype(jnp.int32)
        return kt, jnp.where(wrap, lows[kt], m + 1)

    def body(_, carry):
        kt, m, flat = carry
        pairs = []
        for i in range(UNROLL):
            pairs.append((kt, m))
            kt, m = advance(kt, m)
        for i in range(UNROLL):
            fold(flat[2 * i], flat[2 * i + 1], probs[i])
            probs[i] = weigh(*pairs[i])
        return kt, m, tuple(v for pair in pairs for v in pair)

    nothing = (jnp.int32(0), jnp.int32(row_blocks)) * UNROLL
    steps = (total + UNROLL - 1) // UNROLL + 1
    lax.fori_loop(0, steps, body, (jnp.int32(0), lows[0], nothing))

    chunks = sems.shape[0]
    per_chunk = row_blocks // chunks

    def finish(m, worst):
        totals = acc[m, HEAD_DIM : HEAD_DIM + 1, :]
        staged[m] = (acc[m, :HEAD_DIM, :] * (1.0 / totals)).astype(jnp.bfloat16)
        fine = jnp.logical_and(totals > LEAST_TOTAL, totals < MOST_TOTAL)
        return jnp.maximum(worst, jnp.where(fine, 0.0, 1.0))

    def send(c):
        cut = pl.ds(c * per_chunk, per_chunk)
        return pltpu.make_async_copy(staged.at[cut], out_ref.at[cut], sems.at[c])

    worst = jnp.zeros((1, BLOCK_ROWS), jnp.float32)
    for c in range(chunks):
        worst = lax.fori_loop(c * per_chunk, (c + 1) * per_chunk, finish, worst)
        send(c).start()
    flag[0] = jnp.max(worst)
    for c in range(chunks):
        send(c).wait()

    @pl.when(flag[0] > 0.0)
    def _():
        def redo(m, carry):
            def masked_scores(kt):
                scores = jnp.dot(key_rows(kt), query_rows(m), preferred_element_type=jnp.float32)
                return scores * SCALE, allowed_keys(m, kt)

            def fold_max(kt, peak):
                scores, allowed = masked_scores(kt)
                masked = jnp.where(allowed, scores, -3e38)
                return jnp.maximum(peak, jnp.max(masked, axis=0, keepdims=True))

            peak = lax.fori_loop(
                0, key_tiles, fold_max, jnp.full((1, BLOCK_ROWS), -3e38, jnp.float32)
            )
            acc[m] = jnp.zeros(acc.shape[1:], jnp.float32)

            def fold_sum(kt, inner):
                scores, allowed = masked_scores(kt)
                p = jnp.where(allowed, jnp.exp(jnp.where(allowed, scores - peak, 0.0)), 0.0)
                fold(kt, m, p.astype(jnp.bfloat16))
                return inner

            lax.fori_loop(0, key_tiles, fold_sum, 0)
            totals = acc[m, HEAD_DIM : HEAD_DIM + 1, :]
            staged[m] = (acc[m, :HEAD_DIM, :] * (1.0 / totals)).astype(jnp.bfloat16)
            return carry

        lax.fori_loop(0, row_blocks, redo, 0)
        for c in range(chunks):
            send(c).start()
        for c in range(chunks):
            send(c).wait()


def attend_call(group, starts, counts, arrived, blocks):
    row_blocks = arrived.shape[0]
    patches = row_blocks * 128
    key_tiles = patches // KEY_TILE
    return pl.pallas_call(
        functools.partial(attend_kernel, blocks),
        out_shape=jax.ShapeDtypeStruct((row_blocks, HEAD_DIM, BLOCK_ROWS), jnp.bfloat16),
        in_specs=[smem(), smem(), vmem(), vmem()],
        out_specs=hbm(),
        scratch_shapes=[
            pltpu.VMEM((patches, 128), jnp.bfloat16),
            pltpu.VMEM((key_tiles, HEAD_DIM + SUM_ROWS, KEY_TILE), jnp.bfloat16),
            pltpu.VMEM((KEY_TILE, 128), jnp.int32),
            pltpu.VMEM((row_blocks + 1, HEAD_DIM + SUM_ROWS, BLOCK_ROWS), jnp.float32),
            pltpu.VMEM((UNROLL, KEY_TILE, BLOCK_ROWS), jnp.bfloat16),
            pltpu.VMEM((row_blocks, HEAD_DIM, BLOCK_ROWS), jnp.bfloat16),
            pltpu.SMEM((key_tiles + 2 * UNROLL + 2,), jnp.int32),
            pltpu.SMEM((1,), jnp.float32),
            pltpu.SemaphoreType.DMA((4,)),
        ],
        compiler_params=pltpu.CompilerParams(vmem_limit_bytes=50 * MIB),
        cost_estimate=pl.CostEstimate(
            flops=2 * patches * row_blocks * BLOCK_ROWS * 2 * HEAD_DIM,
            bytes_accessed=2 * 3 * arrived.size // 2,
            transcendentals=patches * row_blocks * BLOCK_ROWS // 2,
        ),
        name="attend",
    )(group, starts, counts, arrived)


OUT_PARTS = 4


def out_kernel(h_ref, w_ref, x_ref, gain_ref, out_ref, weights, acc, staged, ins, outs):
    copies = h_ref.shape[0]
    width = w_ref.shape[0]
    depth = width // OUT_PARTS
    loads = []
    for i in range(OUT_PARTS):
        cut = pl.ds(i * depth, depth)
        loads.append(pltpu.make_async_copy(w_ref.at[cut], weights.at[cut], ins.at[i]))
        loads[i].start()
    for i in range(OUT_PARTS):
        loads[i].wait()
        part = weights[i * depth : (i + 1) * depth, :]
        heads = depth // HEAD_DIM
        for r in range(copies):
            head_out = h_ref[r, i * heads : (i + 1) * heads].reshape(depth, BLOCK_ROWS).T
            product = jnp.dot(head_out, part, preferred_element_type=jnp.float32)
            acc[r] = product if i == 0 else acc[r] + product
    sent = []
    for r in range(copies):
        cut = slice(r * BLOCK_ROWS, (r + 1) * BLOCK_ROWS)
        residual = x_ref[cut, :].astype(jnp.float32) + acc[r]
        staged[cut, :] = norm_rows(residual, gain_ref[...]).astype(jnp.bfloat16)
        where = pl.ds(r * BLOCK_ROWS, BLOCK_ROWS)
        send = pltpu.make_async_copy(staged.at[where], out_ref.at[where], outs.at[r])
        send.start()
        sent.append(send)
    for send in sent:
        send.wait()


def out_call(head_out, w_out, x, gain):
    rows, width = x.shape
    return pl.pallas_call(
        out_kernel,
        out_shape=jax.ShapeDtypeStruct(x.shape, jnp.bfloat16),
        in_specs=[vmem(), hbm(), vmem(), vmem()],
        out_specs=hbm(),
        scratch_shapes=[
            pltpu.VMEM(w_out.shape, jnp.bfloat16),
            pltpu.VMEM((rows // BLOCK_ROWS, BLOCK_ROWS, width), jnp.float32),
            pltpu.VMEM(x.shape, jnp.bfloat16),
            pltpu.SemaphoreType.DMA((OUT_PARTS,)),
            pltpu.SemaphoreType.DMA((rows // BLOCK_ROWS,)),
        ],
        compiler_params=pltpu.CompilerParams(vmem_limit_bytes=50 * MIB),
        cost_estimate=pl.CostEstimate(
            flops=2 * rows * width * width, bytes_accessed=2 * (3 * rows * width + width * width),
            transcendentals=rows,
        ),
        name="outputs",
    )(head_out, w_out, x, gain.reshape(1, -1))


def per_device(
    byte_states, patch_latents, patch_lengths, w_down, kv_gain, w_query, w_key, w_value, w_out,
    out_gain,
):
    seqs, mps = lax.axis_size("seq"), lax.axis_size("mp")
    copies = mps // HEADS
    x = byte_states[0]
    patches_here, features = patch_latents.shape[1:]
    part = patches_here // mps

    sent = patch_latents.reshape(seqs * mps, part, features)
    latents = lax.all_to_all(sent, ("seq", "mp"), 0, 0, tiled=True)
    latents = latents.reshape(seqs, mps, part, features)
    lengths = patch_lengths[0].reshape(-1, 128)
    buf, starts, counts = query_call(x, w_query, lengths, mps * x.shape[0])

    buf = kv_call(latents, w_down, kv_gain, w_key, w_value, buf)
    arrived = lax.all_to_all(buf, "mp", 0, 0, tiled=True)

    group = jnp.stack([lax.axis_index("mp") // HEADS, jnp.int32(copies)])
    head_out = attend_call(group, starts, counts, arrived, seqs)
    head_out = lax.all_to_all(head_out, "mp", 0, 0, tiled=True)
    decoded = out_call(
        head_out.reshape(copies, HEADS, HEAD_DIM, BLOCK_ROWS), w_out, x, out_gain
    )
    return decoded[None]


def solution(mesh):
    return jax.shard_map(
        per_device,
        mesh=mesh,
        in_specs=(
            P("seq", "mp", None),
            P(None, "seq", "mp"),
            P("seq", None),
            P(),
            P(),
            P(),
            P(),
            P(),
            P(),
            P(),
        ),
        out_specs=P("seq", "mp", None),
        check_vma=False,
    )
```

time: 296 us -> 285 us (0.963)
  local copies, waits for them, and re-layouts: 11 us -> 1.61 us
  waiting for transfers between devices: 54.3 us -> 59.8 us
  starting transfers between devices: 26.5 us -> 21.8 us
  Pallas kernels: 203 us -> 200 us
    unnamed x24 -> x10, local copies, waits for them, and re-layouts: 11 us -> 1.6 us
    all_to_all x2 -> x1, starting transfers between devices: 10.9 us -> 5.68 us  [per_device(): arrived = lax.all_to_all(buf, 'mp', 0, 0, tiled=True)]
    pallas_call x3, Pallas kernels: 201 us -> 196 us  [the longest x1 187 us: attend_call(): pl.pallas_call(functools.partial(attend_kernel, blocks), out_shape=jax.Sh...]
    all_to_all x2 -> x1, waiting for transfers between devices: 25.8 us -> 28.7 us  [per_device(): arrived = lax.all_to_all(buf, 'mp', 0, 0, tiled=True)]
  transfers between devices with their start and end apart: 4 -> 3, of which waited for: 4 -> 3; matrix products, arithmetic and copies ran while one was open for 0% -> 0% of each run, Pallas kernels for 2% -> 1%
where the time goes in v2:
time: 285 us; the launch traced here: 283 us
  Pallas kernels  200 us (70%)
  waiting for transfers between devices  59.8 us (21%)
  starting transfers between devices  21.8 us (8%)
    pallas_call x1, Pallas kernels, attend_call(): pl.pallas_call(functools.partial(attend_kernel, blocks), out_shape=jax.Sh...  187 us
    all_to_all x1, waiting for transfers between devices, per_device(): arrived = lax.all_to_all(buf, 'mp', 0, 0, tiled=True)  28.7 us
    all_to_all x1, waiting for transfers between devices, per_device(): head_out = lax.all_to_all(head_out, 'mp', 0, 0, tiled=True)  17.8 us
    all_to_all x1, waiting for transfers between devices, per_device(): latents = lax.all_to_all(sent, ('seq', 'mp'), 0, 0, tiled=True)  13.3 us
    all_to_all x1, starting transfers between devices, per_device(): latents = lax.all_to_all(sent, ('seq', 'mp'), 0, 0, tiled=True)  10.3 us
    pallas_call x1, Pallas kernels, kv_call(): pl.pallas_call(kv_kernel, out_shape=jax.ShapeDtypeStruct(buf.shape, buf.d...  6.34 us
    all_to_all x1, starting transfers between devices, per_device(): head_out = lax.all_to_all(head_out, 'mp', 0, 0, tiled=True)  5.8 us
  transfers between devices with their start and end apart: 3, of which 3 were waited for; matrix products, arithmetic and copies ran while one was open for 0% of the time, Pallas kernels for 1%

profile of v2, /device:TPU:24, one launch (start us, length us, event | category | flops | bytes accessed | tf_op | source)
XLA Modules:
  0.0 283.2 jit_solution(12141552924894103173)
XLA Ops:
  0.0 0.0 copy-start.3
  0.0 0.0 copy-start
  0.0 0.0 copy-start.2
  0.0 10.3 %all-to-all-start = ((bf16[128,32,128]{2,1,0:T(8,128)(2,1)}), bf16[128,32,128]{2,1,0:T(8,128)(2,1)S(1)}, u32[]{:S(2)}, u32[]{:S(2)}) async-start(bf16[128,32,128]{2,1,0:T(8,128)(2,1)} %bitcast.12), calls=%async_computation | async-start | bytes 2097152 | tf_op jit(solution)/shard_map/all_to_all | solution.py:463
  10.3 0.0 copy-done.3
  10.3 0.0 copy-done
  10.3 0.0 copy-done.2
  10.3 0.0 copy-start.1
  10.3 1.6 copy-done.1
  11.9 3.2 %queries.1 = (bf16[32,256,128]{2,1,0:T(8,128)(2,1)}, s32[32,128]{1,0:T(8,128)S(1)}, s32[128,128]{1,0:T(8,128)S(1)}) custom-call(bf16[512,1024]{1,0:T(8,128)(2,1)S(1)} %bitcast.9, bf16[1024,1024]{1,0:T(8,128)(2,1)S(1)} %copy-done.1, s32[32,128]{1,0:T(8,128)S(1)} %bitcast.11), custom_call_target="tpu_custom_call" | custom-call | flops 1073741824 | bytes 4194304 | tf_op jit(solution)/shard_map/queries/pallas_call | solution.py:109
  15.1 13.3 %all-to-all-done = bf16[128,32,128]{2,1,0:T(8,128)(2,1)S(1)} async-done(((bf16[128,32,128]{2,1,0:T(8,128)(2,1)}), bf16[128,32,128]{2,1,0:T(8,128)(2,1)S(1)}, u32[]{:S(2)}, u32[]{:S(2)}) %all-to-all-start) | async-done | bytes 1048608 | tf_op jit(solution)/shard_map/all_to_all | solution.py:463
  28.5 6.3 %keys_values.1 = bf16[32,256,128]{2,1,0:T(8,128)(2,1)} custom-call(bf16[4,32,32,128]{3,2,1,0:T(8,128)(2,1)S(1)} %bitcast.7, bf16[4096,1024]{1,0:T(8,128)(2,1)} %wd_ref.1, bf16[1,1024]{1,0:T(2,128)(2,1)S(1)} %reshape.17.gain_ref, bf16[1024,1024]{1,0:T(8,128)(2,1)} %wk_ref.1, bf16[1024,1024]{1,0:T(8,128)(2,1)} %wv_ref.1, ...), custom_call_target="tpu_custom_call", output_to_operand_aliasing={{}: (5, {})} | custom-call | flops 1610612736 | bytes 13631488 | tf_op jit(solution)/shard_map/keys_values/pallas_call | solution.py:197
  34.8 5.7 %all-to-all-start.1 = ((bf16[32,256,128]{2,1,0:T(8,128)(2,1)}), bf16[32,256,128]{2,1,0:T(8,128)(2,1)S(1)}, u32[]{:S(2)}, u32[]{:S(2)}) async-start(bf16[32,256,128]{2,1,0:T(8,128)(2,1)} %keys_values.1), calls=%async_computation.1 | async-start | bytes 4194304 | tf_op jit(solution)/shard_map/all_to_all | solution.py:469
  40.5 0.1 pad_add_fusion.group_ref
  40.6 28.7 %all-to-all-done.1.in_ref = bf16[32,256,128]{2,1,0:T(8,128)(2,1)S(1)} async-done(((bf16[32,256,128]{2,1,0:T(8,128)(2,1)}), bf16[32,256,128]{2,1,0:T(8,128)(2,1)S(1)}, u32[]{:S(2)}, u32[]{:S(2)}) %all-to-all-start.1) | async-done | bytes 2097184 | tf_op jit(solution)/shard_map/all_to_all | solution.py:469
  69.3 186.7 %attend.1 = bf16[32,64,256]{2,1,0:T(8,128)(2,1)} custom-call(s32[2]{0:T(128)S(1)} %pad_add_fusion.group_ref, s32[32,128]{1,0:T(8,128)S(1)} %get-tuple-element.8.starts_ref, s32[128,128]{1,0:T(8,128)S(1)} %get-tuple-element.9.counts_ref, bf16[32,256,128]{2,1,0:T(8,128)(2,1)S(1)} %all-to-all-done.1.in_ref), custom_call_target="tpu_custom_call" | custom-call | flops 8589934592 | bytes 3145728 | tf_op jit(solution)/shard_map/attend/pallas_call | solution.py:370
  256.0 0.0 copy-start.4
  256.0 5.8 %all-to-all-start.2 = ((bf16[32,64,256]{2,1,0:T(8,128)(2,1)}), bf16[32,64,256]{2,1,0:T(8,128)(2,1)S(1)}, u32[]{:S(2)}, u32[]{:S(2)}) async-start(bf16[32,64,256]{2,1,0:T(8,128)(2,1)} %attend.1), calls=%async_computation.2 | async-start | bytes 2097152 | tf_op jit(solution)/shard_map/all_to_all | solution.py:473
  261.8 0.0 copy-done.4
  261.8 17.8 %all-to-all-done.2 = bf16[32,64,256]{2,1,0:T(8,128)(2,1)S(1)} async-done(((bf16[32,64,256]{2,1,0:T(8,128)(2,1)}), bf16[32,64,256]{2,1,0:T(8,128)(2,1)S(1)}, u32[]{:S(2)}, u32[]{:S(2)}) %all-to-all-start.2) | async-done | bytes 1048608 | tf_op jit(solution)/shard_map/all_to_all | solution.py:473
  279.6 3.6 %outputs.1 = bf16[512,1024]{1,0:T(8,128)(2,1)} custom-call(bf16[2,16,64,256]{3,2,1,0:T(8,128)(2,1)S(1)} %bitcast.8, bf16[1024,1024]{1,0:T(8,128)(2,1)} %w_ref.3, bf16[512,1024]{1,0:T(8,128)(2,1)S(1)} %bitcast.10, bf16[1,1024]{1,0:T(2,128)(2,1)S(1)} %reshape.19.gain_ref), custom_call_target="tpu_custom_call" | custom-call | flops 1073741824 | bytes 5242880 | tf_op jit(solution)/shard_map/outputs/pallas_call | solution.py:431
  (2 shorter events, 0.0 us)
Async XLA Ops:
  0.0 10.3 %copy-start.3 = (bf16[1024]{0:T(1024)(128)(2,1)S(1)}, bf16[1024]{0:T(1024)(128)(2,1)}, u32[]{:S(2)}) copy-start(bf16[1024]{0:T(1024)(128)(2,1)} %param.14) | copy-start | bytes 6148
  0.0 10.3 %copy-start = (bf16[1,512,1024]{2,1,0:T(8,128)(2,1)S(1)}, bf16[1,512,1024]{2,1,0:T(8,128)(2,1)}, u32[]{:S(2)}) copy-start(bf16[1,512,1024]{2,1,0:T(8,128)(2,1)} %param.10) | copy-start | bytes 3145732
  0.0 10.3 %copy-start.2 = (s32[1,4096]{1,0:T(1,128)S(1)}, s32[1,4096]{1,0:T(1,128)}, u32[]{:S(2)}) copy-start(s32[1,4096]{1,0:T(1,128)} %param.12) | copy-start | bytes 49156
  0.0 28.4 %all-to-all-start = ((bf16[128,32,128]{2,1,0:T(8,128)(2,1)}), bf16[128,32,128]{2,1,0:T(8,128)(2,1)S(1)}, u32[]{:S(2)}, u32[]{:S(2)}) async-start(bf16[128,32,128]{2,1,0:T(8,128)(2,1)} %bitcast.12), calls=%async_computation | async-start | bytes 2097152 | tf_op jit(solution)/shard_map/all_to_all | solution.py:463
  10.3 1.6 copy-start.1
  34.8 34.5 %all-to-all-start.1 = ((bf16[32,256,128]{2,1,0:T(8,128)(2,1)}), bf16[32,256,128]{2,1,0:T(8,128)(2,1)S(1)}, u32[]{:S(2)}, u32[]{:S(2)}) async-start(bf16[32,256,128]{2,1,0:T(8,128)(2,1)} %keys_values.1), calls=%async_computation.1 | async-start | bytes 4194304 | tf_op jit(solution)/shard_map/all_to_all | solution.py:469
  256.0 5.8 %copy-start.4 = (bf16[1024]{0:T(1024)(128)(2,1)S(1)}, bf16[1024]{0:T(1024)(128)(2,1)}, u32[]{:S(2)}) copy-start(bf16[1024]{0:T(1024)(128)(2,1)} %param.19) | copy-start | bytes 6148
  256.0 23.6 %all-to-all-start.2 = ((bf16[32,64,256]{2,1,0:T(8,128)(2,1)}), bf16[32,64,256]{2,1,0:T(8,128)(2,1)S(1)}, u32[]{:S(2)}, u32[]{:S(2)}) async-start(bf16[32,64,256]{2,1,0:T(8,128)(2,1)} %attend.1), calls=%async_computation.2 | async-start | bytes 2097152 | tf_op jit(solution)/shard_map/all_to_all | solution.py:473

commit v3 on v2

--- a/solution.py
+++ b/solution.py
@@ -12,7 +12,7 @@
 HEAD_DIM = 64
 BLOCK_ROWS = 256
 KEY_TILE = 512
-UNROLL = 8
+UNROLL = 6
 SUM_ROWS = 16
 TO_LOG2 = math.log2(math.e) / math.sqrt(HEAD_DIM)
 SCALE = 1.0 / math.sqrt(HEAD_DIM)
@@ -134,6 +134,7 @@
 
 
 WD_PARTS = 8
+AHEAD = 5
 
 
 def kv_kernel(
@@ -151,9 +152,11 @@
     ]
     loads.append(pltpu.make_async_copy(wk_ref, wk, sems.at[WD_PARTS]))
     loads.append(pltpu.make_async_copy(wv_ref, wv, sems.at[WD_PARTS + 1]))
-    for load in loads:
+    for load in loads[:AHEAD]:
         load.start()
     for i in range(WD_PARTS):
+        if i + AHEAD < len(loads):
+            loads[i + AHEAD].start()
         lhs = jnp.concatenate(
             [x_ref[:, i * per_part + g].reshape(rows, lanes) for g in range(per_part)], axis=1
         )
@@ -162,6 +165,8 @@
             lhs, wd[i * depth : (i + 1) * depth, :], preferred_element_type=jnp.float32
         )
         acc[...] = product if i == 0 else acc[...] + product
+    for load in loads[WD_PARTS + AHEAD :]:
+        load.start()
     normed = norm_rows(acc[...], gain_ref[...]).astype(jnp.bfloat16)
     loads[WD_PARTS].wait()
     loads[WD_PARTS + 1].wait()
@@ -219,10 +224,24 @@
     )(x, w_down, gain.reshape(1, -1), w_key, w_value, buf)
 
 
-def attend_kernel(
-    blocks, group_ref, starts_ref, counts_ref, in_ref, out_ref,
-    kvs, vt, order, acc, probs, staged, lows, flag, sems,
-):
+def stage(rhs, register, mxu):
+    pltpu.matmul_push_rhs(rhs, staging_register=register, mxu_index=mxu)
+
+
+def attend_kernel(blocks, *refs):
+    unit = KEY_TILE // 2
+    kinds = []
+    for mxu in range(2):
+        kinds += [pltpu.ACC(mxu)((unit, BLOCK_ROWS), jnp.float32)] * 3
+        kinds += [pltpu.ACC(mxu)((HEAD_DIM + SUM_ROWS, BLOCK_ROWS), jnp.float32)] * 3
+    pl.run_scoped(functools.partial(attend_body, blocks, refs), *kinds)
+
+
+def attend_body(blocks, refs, *accs):
+    group_ref, starts_ref, counts_ref, in_ref, out_ref = refs[:5]
+    kvs, vt, order, acc, probs, staged, split, lows, flag, sems = refs[5:]
+    score_accs, sum_accs = (accs[0:3], accs[6:9]), (accs[3:6], accs[9:12])
+    unit = KEY_TILE // 2
     row_blocks = in_ref.shape[0]
     senders = row_blocks
     part = 128 // blocks
@@ -248,64 +267,139 @@
         for s in range(senders):
             at = (b * senders + s) * part
             kvs[at : at + part, :] = in_ref[s, b * part : (b + 1) * part, :]
+    sum_row = ones_where(iota((SUM_ROWS, KEY_TILE), 0) == 0)
     for t in range(key_tiles):
         turned = kvs[t * KEY_TILE : (t + 1) * KEY_TILE, :].T
         vt[t, :HEAD_DIM, :] = turned[HEAD_DIM:, :]
-        vt[t, HEAD_DIM:, :] = jnp.ones((SUM_ROWS, KEY_TILE), jnp.bfloat16)
-    order[...] = iota(order.shape, 0)
-
-    def clear(m, carry):
-        acc[m] = jnp.zeros(acc.shape[1:], jnp.float32)
-        return carry
-
-    lax.fori_loop(0, row_blocks + 1, clear, 0)
-    zeros = jnp.zeros((HEAD_DIM, BLOCK_ROWS), jnp.bfloat16)
+        vt[t, HEAD_DIM:, :] = sum_row
+        own = kvs[t * KEY_TILE : (t + 1) * KEY_TILE, :HEAD_DIM]
+        kvs[t * KEY_TILE : (t + 1) * KEY_TILE, :] = jnp.concatenate([own, own], axis=1)
+    order[...] = iota(order.shape, 0).astype(jnp.float32).astype(jnp.bfloat16)
+
+    blank = jnp.zeros((unit, 128), jnp.bfloat16)
     lanes = BLOCK_ROWS // 128
 
-    def query_rows(m):
+    def prepare(m, carry):
         halves = [
             in_ref[m, 128 + b * HEAD_DIM : 128 + (b + 1) * HEAD_DIM, :] for b in range(lanes)
         ]
+        scaled = jnp.concatenate(halves, axis=1).astype(jnp.float32) * TO_LOG2
+        high = scaled.astype(jnp.bfloat16)
+        split[m, :HEAD_DIM, :] = high
+        split[m, HEAD_DIM:, :] = (scaled - high.astype(jnp.float32)).astype(jnp.bfloat16)
+        acc[m] = jnp.zeros(acc.shape[1:], jnp.float32)
+        return carry
+
+    lax.fori_loop(0, row_blocks, prepare, 0)
+    acc[row_blocks] = jnp.zeros(acc.shape[1:], jnp.float32)
+
+    def query_rows(m):
+        return jnp.concatenate([split[m], jnp.zeros((128, BLOCK_ROWS), jnp.bfloat16)], axis=0)
+
+    def exact_query_rows(m):
+        halves = [
+            in_ref[m, 128 + b * HEAD_DIM : 128 + (b + 1) * HEAD_DIM, :] for b in range(lanes)
+        ]
+        zeros = jnp.zeros((256 - HEAD_DIM, BLOCK_ROWS), jnp.bfloat16)
         return jnp.concatenate([jnp.concatenate(halves, axis=1), zeros], axis=0)
 
-    def allowed_keys(m, kt):
+    def last_keys(m):
         line = (m * stride + group * BLOCK_ROWS) // 128
         met = [counts_ref[pl.ds(line + b, 1), :] for b in range(lanes)]
-        here = jnp.concatenate(met, axis=1) - kt * KEY_TILE
-        return jnp.concatenate([order[...]] * lanes, axis=1) < here
-
-    def key_rows(kt):
-        return kvs[pl.ds(pl.multiple_of(kt * KEY_TILE, KEY_TILE), KEY_TILE), :]
-
-    def weigh(kt, m):
-        kt, m = jnp.minimum(kt, key_tiles - 1), jnp.minimum(m, row_blocks - 1)
-        scores = jnp.dot(key_rows(kt), query_rows(m), preferred_element_type=jnp.float32)
-        p = jnp.where(allowed_keys(m, kt), jnp.exp2(scores * TO_LOG2), 0.0)
-        return p.astype(jnp.bfloat16)
-
-    def fold(kt, m, p):
-        kt = jnp.minimum(kt, key_tiles - 1)
-        acc[m] = acc[m] + jnp.dot(vt[kt], p, preferred_element_type=jnp.float32)
+        return jnp.concatenate(met, axis=1)
+
+    def allowed_keys(m, kt, part):
+        met = jnp.clip(last_keys(m) - (kt * KEY_TILE + part * unit), 0, unit)
+        met = met.astype(jnp.float32).astype(jnp.bfloat16)
+        return jnp.concatenate([order[...]] * lanes, axis=1) < met
+
+    def key_rows(kt, part):
+        at = pl.multiple_of(kt * KEY_TILE + part * unit, unit)
+        return jnp.concatenate([kvs[pl.ds(at, unit), :], blank], axis=1)
+
+    def value_columns(kt, part):
+        return vt[kt, :, part * unit : (part + 1) * unit]
+
+    def inside(kt, m):
+        return jnp.minimum(kt, key_tiles - 1), jnp.minimum(m, row_blocks - 1)
 
     def advance(kt, m):
         wrap = m + 1 >= row_blocks
         kt = kt + wrap.astype(jnp.int32)
         return kt, jnp.where(wrap, lows[kt], m + 1)
 
+    def ring(i, part):
+        return score_accs[i % 2][(2 * (i // 2) + part) % 3]
+
+    def total_of(i):
+        return sum_accs[i % 2][(i // 2) % 3]
+
+    def settle_scores(i, part, kt, m):
+        p = jnp.exp2(pltpu.matmul_pop(ring(i, part))).astype(jnp.bfloat16)
+        p = jnp.where(allowed_keys(m, kt, part), p, jnp.zeros_like(p))
+        probs[i, part * unit : (part + 1) * unit] = p
+
+    def settle_sums(i, m):
+        acc[m] = acc[m] + pltpu.matmul_pop(total_of(i))
+
+    def stage_first(kt, m):
+        for mxu in range(2):
+            stage(query_rows(inside(kt, m)[1]), 0, mxu)
+            kt, m = advance(kt, m)
+
     def body(_, carry):
-        kt, m, flat = carry
+        kt, m, old, open_sums = carry
         pairs = []
         for i in range(UNROLL):
-            pairs.append((kt, m))
+            pairs.append(inside(kt, m) + (m,))
             kt, m = advance(kt, m)
-        for i in range(UNROLL):
-            fold(flat[2 * i], flat[2 * i + 1], probs[i])
-            probs[i] = weigh(*pairs[i])
-        return kt, m, tuple(v for pair in pairs for v in pair)
-
-    nothing = (jnp.int32(0), jnp.int32(row_blocks)) * UNROLL
+        for j in range(0, UNROLL, 2):
+            now = (j, j + 1)
+            if j == 0:
+                before = [
+                    (i, old[3 * i], old[3 * i + 1], open_sums[i - UNROLL + 2])
+                    for i in (UNROLL - 2, UNROLL - 1)
+                ]
+            else:
+                before = [(i, pairs[i][0], pairs[i][1], old[3 * i + 2]) for i in (j - 2, j - 1)]
+            for i in now:
+                pltpu.matmul_acc_lhs(ring(i, 0), key_rows(pairs[i][0], 0), load_staged_rhs=0)
+                stage(probs[i, :unit], 0, i % 2)
+                stage(probs[i, unit:], 1, i % 2)
+            for i, b_kt, b_m, _ in before:
+                settle_scores(i, 0, b_kt, b_m)
+            for i in now:
+                pltpu.matmul_acc_lhs(ring(i, 1), key_rows(pairs[i][0], 1))
+            for i, b_kt, b_m, _ in before:
+                settle_scores(i, 1, b_kt, b_m)
+            for i in now:
+                old_kt = old[3 * i]
+                pltpu.matmul_acc_lhs(total_of(i), value_columns(old_kt, 0), load_staged_rhs=0)
+                if i + 2 < UNROLL:
+                    stage(query_rows(pairs[i + 2][1]), 0, i % 2)
+                pltpu.matmul_acc_lhs(total_of(i), value_columns(old_kt, 1), load_staged_rhs=1)
+            for i, _, _, b_m in before:
+                settle_sums(i, b_m)
+        stage_first(kt, m)
+        now_open = tuple(old[3 * i + 2] for i in (UNROLL - 2, UNROLL - 1))
+        return kt, m, tuple(v for pair in pairs for v in pair), now_open
+
+    trash = jnp.int32(row_blocks)
+    nothing = (jnp.int32(0), jnp.int32(0), trash) * UNROLL
     steps = (total + UNROLL - 1) // UNROLL + 1
-    lax.fori_loop(0, steps, body, (jnp.int32(0), lows[0], nothing))
+    for spare in accs:
+        probs[0, : spare.shape[0]] = pltpu.matmul_pop(spare).astype(jnp.bfloat16)
+    first = (jnp.int32(0), lows[0])
+    stage_first(*first)
+    kt, m, _, open_sums = lax.fori_loop(0, steps, body, first + (nothing, (trash, trash)))
+    for i in (UNROLL - 2, UNROLL - 1):
+        settle_sums(i, open_sums[i - UNROLL + 2])
+        for part in range(2):
+            probs[i, part * unit : (part + 1) * unit] = pltpu.matmul_pop(ring(i, part)).astype(
+                jnp.bfloat16
+            )
+        pltpu.matmul_acc_lhs(ring(i, 0), jnp.zeros((unit, 256), jnp.bfloat16), load_staged_rhs=0)
+        probs[i, :unit] = pltpu.matmul_pop(ring(i, 0)).astype(jnp.bfloat16)
 
     chunks = sems.shape[0]
     per_chunk = row_blocks // chunks
@@ -332,13 +426,21 @@
     def _():
         def redo(m, carry):
             def masked_scores(kt):
-                scores = jnp.dot(key_rows(kt), query_rows(m), preferred_element_type=jnp.float32)
-                return scores * SCALE, allowed_keys(m, kt)
+                stage(exact_query_rows(m), 0, 0)
+                pltpu.matmul_acc_lhs(score_accs[0][0], key_rows(kt, 0), load_staged_rhs=0)
+                pltpu.matmul_acc_lhs(score_accs[0][1], key_rows(kt, 1))
+                parts = []
+                for part in range(2):
+                    scores = pltpu.matmul_pop(score_accs[0][part]) * SCALE
+                    met = jnp.clip(last_keys(m) - (kt * KEY_TILE + part * unit), 0, unit)
+                    parts.append((scores, iota((unit, BLOCK_ROWS), 0) < met))
+                return parts
 
             def fold_max(kt, peak):
-                scores, allowed = masked_scores(kt)
-                masked = jnp.where(allowed, scores, -3e38)
-                return jnp.maximum(peak, jnp.max(masked, axis=0, keepdims=True))
+                for scores, allowed in masked_scores(kt):
+                    masked = jnp.where(allowed, scores, -3e38)
+                    peak = jnp.maximum(peak, jnp.max(masked, axis=0, keepdims=True))
+                return peak
 
             peak = lax.fori_loop(
                 0, key_tiles, fold_max, jnp.full((1, BLOCK_ROWS), -3e38, jnp.float32)
@@ -346,9 +448,13 @@
             acc[m] = jnp.zeros(acc.shape[1:], jnp.float32)
 
             def fold_sum(kt, inner):
-                scores, allowed = masked_scores(kt)
-                p = jnp.where(allowed, jnp.exp(jnp.where(allowed, scores - peak, 0.0)), 0.0)
-                fold(kt, m, p.astype(jnp.bfloat16))
+                for part, (scores, allowed) in enumerate(masked_scores(kt)):
+                    p = jnp.where(allowed, jnp.exp(jnp.where(allowed, scores - peak, 0.0)), 0.0)
+                    stage(p.astype(jnp.bfloat16), 0, 0)
+                    pltpu.matmul_acc_lhs(
+                        sum_accs[0][0], value_columns(kt, part), load_staged_rhs=0
+                    )
+                acc[m] = acc[m] + pltpu.matmul_pop(sum_accs[0][0])
                 return inner
 
             lax.fori_loop(0, key_tiles, fold_sum, 0)
@@ -375,10 +481,11 @@
         scratch_shapes=[
             pltpu.VMEM((patches, 128), jnp.bfloat16),
             pltpu.VMEM((key_tiles, HEAD_DIM + SUM_ROWS, KEY_TILE), jnp.bfloat16),
-            pltpu.VMEM((KEY_TILE, 128), jnp.int32),
+            pltpu.VMEM((KEY_TILE // 2, 128), jnp.bfloat16),
             pltpu.VMEM((row_blocks + 1, HEAD_DIM + SUM_ROWS, BLOCK_ROWS), jnp.float32),
             pltpu.VMEM((UNROLL, KEY_TILE, BLOCK_ROWS), jnp.bfloat16),
             pltpu.VMEM((row_blocks, HEAD_DIM, BLOCK_ROWS), jnp.bfloat16),
+            pltpu.VMEM((row_blocks, 2 * HEAD_DIM, BLOCK_ROWS), jnp.bfloat16),
             pltpu.SMEM((key_tiles + 2 * UNROLL + 2,), jnp.int32),
             pltpu.SMEM((1,), jnp.float32),
             pltpu.SemaphoreType.DMA((4,)),

time: 285 us -> 304 us (1.067)
  Pallas kernels: 200 us -> 220 us
    pallas_call x1, Pallas kernels: 187 us -> 206 us  [attend_call(): pl.pallas_call(functools.partial(attend_kernel, blocks), out_shape=jax.Sh...]
where the time goes in v3:
time: 304 us; the launch traced here: 303 us
  Pallas kernels  220 us (72%)
  waiting for transfers between devices  59.4 us (20%)
  starting transfers between devices  21.8 us (7%)
    pallas_call x1, Pallas kernels, attend_call(): pl.pallas_call(functools.partial(attend_kernel, blocks), out_shape=jax.Sh...  206 us
    all_to_all x1, waiting for transfers between devices, per_device(): arrived = lax.all_to_all(buf, 'mp', 0, 0, tiled=True)  28.7 us
    all_to_all x1, waiting for transfers between devices, per_device(): head_out = lax.all_to_all(head_out, 'mp', 0, 0, tiled=True)  17.4 us
    all_to_all x1, waiting for transfers between devices, per_device(): latents = lax.all_to_all(sent, ('seq', 'mp'), 0, 0, tiled=True)  13.3 us
    all_to_all x1, starting transfers between devices, per_device(): latents = lax.all_to_all(sent, ('seq', 'mp'), 0, 0, tiled=True)  10.3 us
    pallas_call x1, Pallas kernels, kv_call(): pl.pallas_call(kv_kernel, out_shape=jax.ShapeDtypeStruct(buf.shape, buf.d...  6.51 us
  transfers between devices with their start and end apart: 3, of which 3 were waited for; matrix products, arithmetic and copies ran while one was open for 0% of the time, Pallas kernels for 1%

profile of v3, /device:TPU:24, one launch (start us, length us, event | category | flops | bytes accessed | tf_op | source)
XLA Modules:
  0.0 302.8 jit_solution(3555866591175019582)
XLA Ops:
  0.0 0.0 copy-start.3
  0.0 0.0 copy-start
  0.0 0.0 copy-start.2
  0.0 10.3 %all-to-all-start = ((bf16[128,32,128]{2,1,0:T(8,128)(2,1)}), bf16[128,32,128]{2,1,0:T(8,128)(2,1)S(1)}, u32[]{:S(2)}, u32[]{:S(2)}) async-start(bf16[128,32,128]{2,1,0:T(8,128)(2,1)} %bitcast.12), calls=%async_computation | async-start | bytes 2097152 | tf_op jit(solution)/shard_map/all_to_all | solution.py:570
  10.3 0.0 copy-done.3
  10.3 0.0 copy-done
  10.3 0.0 copy-done.2
  10.3 0.0 copy-start.1
  10.3 1.6 copy-done.1
  11.9 3.2 %queries.1 = (bf16[32,256,128]{2,1,0:T(8,128)(2,1)}, s32[32,128]{1,0:T(8,128)S(1)}, s32[128,128]{1,0:T(8,128)S(1)}) custom-call(bf16[512,1024]{1,0:T(8,128)(2,1)S(1)} %bitcast.9, bf16[1024,1024]{1,0:T(8,128)(2,1)S(1)} %copy-done.1, s32[32,128]{1,0:T(8,128)S(1)} %bitcast.11), custom_call_target="tpu_custom_call" | custom-call | flops 1073741824 | bytes 4194304 | tf_op jit(solution)/shard_map/queries/pallas_call | solution.py:109
  15.1 13.3 %all-to-all-done = bf16[128,32,128]{2,1,0:T(8,128)(2,1)S(1)} async-done(((bf16[128,32,128]{2,1,0:T(8,128)(2,1)}), bf16[128,32,128]{2,1,0:T(8,128)(2,1)S(1)}, u32[]{:S(2)}, u32[]{:S(2)}) %all-to-all-start) | async-done | bytes 1048608 | tf_op jit(solution)/shard_map/all_to_all | solution.py:570
  28.5 6.5 %keys_values.1 = bf16[32,256,128]{2,1,0:T(8,128)(2,1)} custom-call(bf16[4,32,32,128]{3,2,1,0:T(8,128)(2,1)S(1)} %bitcast.7, bf16[4096,1024]{1,0:T(8,128)(2,1)} %wd_ref.1, bf16[1,1024]{1,0:T(2,128)(2,1)S(1)} %reshape.17.gain_ref, bf16[1024,1024]{1,0:T(8,128)(2,1)} %wk_ref.1, bf16[1024,1024]{1,0:T(8,128)(2,1)} %wv_ref.1, ...), custom_call_target="tpu_custom_call", output_to_operand_aliasing={{}: (5, {})} | custom-call | flops 1610612736 | bytes 13631488 | tf_op jit(solution)/shard_map/keys_values/pallas_call | solution.py:202
  35.0 5.7 %all-to-all-start.1 = ((bf16[32,256,128]{2,1,0:T(8,128)(2,1)}), bf16[32,256,128]{2,1,0:T(8,128)(2,1)S(1)}, u32[]{:S(2)}, u32[]{:S(2)}) async-start(bf16[32,256,128]{2,1,0:T(8,128)(2,1)} %keys_values.1), calls=%async_computation.1 | async-start | bytes 4194304 | tf_op jit(solution)/shard_map/all_to_all | solution.py:576
  40.7 0.1 pad_add_fusion.refs_0_
  40.8 28.7 %all-to-all-done.1.refs_3_ = bf16[32,256,128]{2,1,0:T(8,128)(2,1)S(1)} async-done(((bf16[32,256,128]{2,1,0:T(8,128)(2,1)}), bf16[32,256,128]{2,1,0:T(8,128)(2,1)S(1)}, u32[]{:S(2)}, u32[]{:S(2)}) %all-to-all-start.1) | async-done | bytes 2097184 | tf_op jit(solution)/shard_map/all_to_all | solution.py:576
  69.5 206.5 %attend.1 = bf16[32,64,256]{2,1,0:T(8,128)(2,1)} custom-call(s32[2]{0:T(128)S(1)} %pad_add_fusion.refs_0_, s32[32,128]{1,0:T(8,128)S(1)} %get-tuple-element.8.refs_1_, s32[128,128]{1,0:T(8,128)S(1)} %get-tuple-element.9.refs_2_, bf16[32,256,128]{2,1,0:T(8,128)(2,1)S(1)} %all-to-all-done.1.refs_3_), custom_call_target="tpu_custom_call" | custom-call | flops 8589934592 | bytes 3145728 | tf_op jit(solution)/shard_map/attend/pallas_call | solution.py:476
  275.9 0.0 copy-start.4
  276.0 5.8 %all-to-all-start.2 = ((bf16[32,64,256]{2,1,0:T(8,128)(2,1)}), bf16[32,64,256]{2,1,0:T(8,128)(2,1)S(1)}, u32[]{:S(2)}, u32[]{:S(2)}) async-start(bf16[32,64,256]{2,1,0:T(8,128)(2,1)} %attend.1), calls=%async_computation.2 | async-start | bytes 2097152 | tf_op jit(solution)/shard_map/all_to_all | solution.py:580
  281.8 0.0 copy-done.4
  281.8 17.4 %all-to-all-done.2 = bf16[32,64,256]{2,1,0:T(8,128)(2,1)S(1)} async-done(((bf16[32,64,256]{2,1,0:T(8,128)(2,1)}), bf16[32,64,256]{2,1,0:T(8,128)(2,1)S(1)}, u32[]{:S(2)}, u32[]{:S(2)}) %all-to-all-start.2) | async-done | bytes 1048608 | tf_op jit(solution)/shard_map/all_to_all | solution.py:580
  299.2 3.6 %outputs.1 = bf16[512,1024]{1,0:T(8,128)(2,1)} custom-call(bf16[2,16,64,256]{3,2,1,0:T(8,128)(2,1)S(1)} %bitcast.8, bf16[1024,1024]{1,0:T(8,128)(2,1)} %w_ref.3, bf16[512,1024]{1,0:T(8,128)(2,1)S(1)} %bitcast.10, bf16[1,1024]{1,0:T(2,128)(2,1)S(1)} %reshape.19.gain_ref), custom_call_target="tpu_custom_call" | custom-call | flops 1073741824 | bytes 5242880 | tf_op jit(solution)/shard_map/outputs/pallas_call | solution.py:538
  (2 shorter events, 0.0 us)
Async XLA Ops:
  0.0 10.3 %copy-start.3 = (bf16[1024]{0:T(1024)(128)(2,1)S(1)}, bf16[1024]{0:T(1024)(128)(2,1)}, u32[]{:S(2)}) copy-start(bf16[1024]{0:T(1024)(128)(2,1)} %param.14) | copy-start | bytes 6148
  0.0 10.3 %copy-start = (bf16[1,512,1024]{2,1,0:T(8,128)(2,1)S(1)}, bf16[1,512,1024]{2,1,0:T(8,128)(2,1)}, u32[]{:S(2)}) copy-start(bf16[1,512,1024]{2,1,0:T(8,128)(2,1)} %param.10) | copy-start | bytes 3145732
  0.0 10.3 %copy-start.2 = (s32[1,4096]{1,0:T(1,128)S(1)}, s32[1,4096]{1,0:T(1,128)}, u32[]{:S(2)}) copy-start(s32[1,4096]{1,0:T(1,128)} %param.12) | copy-start | bytes 49156
  0.0 28.4 %all-to-all-start = ((bf16[128,32,128]{2,1,0:T(8,128)(2,1)}), bf16[128,32,128]{2,1,0:T(8,128)(2,1)S(1)}, u32[]{:S(2)}, u32[]{:S(2)}) async-start(bf16[128,32,128]{2,1,0:T(8,128)(2,1)} %bitcast.12), calls=%async_computation | async-start | bytes 2097152 | tf_op jit(solution)/shard_map/all_to_all | solution.py:570
  10.3 1.6 copy-start.1
  35.0 34.5 %all-to-all-start.1 = ((bf16[32,256,128]{2,1,0:T(8,128)(2,1)}), bf16[32,256,128]{2,1,0:T(8,128)(2,1)S(1)}, u32[]{:S(2)}, u32[]{:S(2)}) async-start(bf16[32,256,128]{2,1,0:T(8,128)(2,1)} %keys_values.1), calls=%async_computation.1 | async-start | bytes 4194304 | tf_op jit(solution)/shard_map/all_to_all | solution.py:576
  275.9 5.8 %copy-start.4 = (bf16[1024]{0:T(1024)(128)(2,1)S(1)}, bf16[1024]{0:T(1024)(128)(2,1)}, u32[]{:S(2)}) copy-start(bf16[1024]{0:T(1024)(128)(2,1)} %param.19) | copy-start | bytes 6148
  276.0 23.2 %all-to-all-start.2 = ((bf16[32,64,256]{2,1,0:T(8,128)(2,1)}), bf16[32,64,256]{2,1,0:T(8,128)(2,1)S(1)}, u32[]{:S(2)}, u32[]{:S(2)}) async-start(bf16[32,64,256]{2,1,0:T(8,128)(2,1)} %attend.1), calls=%async_computation.2 | async-start | bytes 2097152 | tf_op jit(solution)/shard_map/all_to_all | solution.py:580

commit v4 on v3

--- a/solution.py
+++ b/solution.py
@@ -71,13 +71,17 @@
     counts_ref[...] = (along + jnp.sum(before, axis=1, keepdims=True)).astype(jnp.int32)
 
 
-def query_kernel(x_ref, w_ref, len_ref, buf_ref, starts_ref, counts_ref, staged, sems):
+def query_kernel(
+    x_ref, w_ref, len_ref, buf_ref, starts_ref, counts_ref, kept_ref, staged, sems, keep_sem
+):
     rows, width = x_ref.shape
     step = 256
     heads_step = step // HEAD_DIM
     copies = rows // BLOCK_ROWS
     half = BLOCK_ROWS // 128
-    sent = []
+    keep = pltpu.make_async_copy(x_ref, kept_ref, keep_sem.at[0])
+    keep.start()
+    sent = [keep]
     for n in range(width // step):
         q = jnp.dot(
             x_ref[...], w_ref[:, n * step : (n + 1) * step], preferred_element_type=jnp.float32
@@ -112,12 +116,14 @@
             jax.ShapeDtypeStruct((copies * HEADS, 256, 128), jnp.bfloat16),
             jax.ShapeDtypeStruct(lengths.shape, jnp.int32),
             jax.ShapeDtypeStruct((seq_len // 128, 128), jnp.int32),
+            jax.ShapeDtypeStruct(x.shape, x.dtype),
         ),
         in_specs=[vmem(), vmem(), vmem()],
-        out_specs=(hbm(), vmem(), vmem()),
+        out_specs=(hbm(), vmem(), vmem(), hbm()),
         scratch_shapes=[
             pltpu.VMEM((copies, HEADS, 128, 128), jnp.bfloat16),
             pltpu.SemaphoreType.DMA((copies * width // 256,)),
+            pltpu.SemaphoreType.DMA((1,)),
         ],
         compiler_params=pltpu.CompilerParams(vmem_limit_bytes=16 * MIB),
         cost_estimate=pl.CostEstimate(
@@ -168,15 +174,16 @@
     for load in loads[WD_PARTS + AHEAD :]:
         load.start()
     normed = norm_rows(acc[...], gain_ref[...]).astype(jnp.bfloat16)
-    loads[WD_PARTS].wait()
-    loads[WD_PARTS + 1].wait()
     copies = buf_ref.shape[0] // HEADS
     step = 256
     heads_step = step // HEAD_DIM
+    loads[WD_PARTS].wait()
+    acc[...] = jnp.dot(normed, wk[...], preferred_element_type=jnp.float32)
+    loads[WD_PARTS + 1].wait()
     sent = []
-    for n in range(wk.shape[1] // step):
+    for n in range(wv.shape[1] // step):
         cut = slice(n * step, (n + 1) * step)
-        keys = jnp.dot(normed, wk[:, cut], preferred_element_type=jnp.float32)
+        keys = acc[:, cut]
         values = jnp.dot(normed, wv[:, cut], preferred_element_type=jnp.float32)
         for h in range(heads_step):
             own = slice(h * HEAD_DIM, (h + 1) * HEAD_DIM)
@@ -239,7 +246,7 @@
 
 def attend_body(blocks, refs, *accs):
     group_ref, starts_ref, counts_ref, in_ref, out_ref = refs[:5]
-    kvs, vt, order, acc, probs, staged, split, lows, flag, sems = refs[5:]
+    kvs, vt, order, acc, probs, split, lows, flag = refs[5:]
     score_accs, sum_accs = (accs[0:3], accs[6:9]), (accs[3:6], accs[9:12])
     unit = KEY_TILE // 2
     row_blocks = in_ref.shape[0]
@@ -272,11 +279,8 @@
         turned = kvs[t * KEY_TILE : (t + 1) * KEY_TILE, :].T
         vt[t, :HEAD_DIM, :] = turned[HEAD_DIM:, :]
         vt[t, HEAD_DIM:, :] = sum_row
-        own = kvs[t * KEY_TILE : (t + 1) * KEY_TILE, :HEAD_DIM]
-        kvs[t * KEY_TILE : (t + 1) * KEY_TILE, :] = jnp.concatenate([own, own], axis=1)
     order[...] = iota(order.shape, 0).astype(jnp.float32).astype(jnp.bfloat16)
 
-    blank = jnp.zeros((unit, 128), jnp.bfloat16)
     lanes = BLOCK_ROWS // 128
 
     def prepare(m, carry):
@@ -290,11 +294,20 @@
         acc[m] = jnp.zeros(acc.shape[1:], jnp.float32)
         return carry
 
-    lax.fori_loop(0, row_blocks, prepare, 0)
+    def four(step):
+        def steps(i, carry):
+            for k in range(4):
+                carry = step(4 * i + k, carry)
+            return carry
+
+        return steps
+
+    lax.fori_loop(0, row_blocks // 4, four(prepare), 0)
     acc[row_blocks] = jnp.zeros(acc.shape[1:], jnp.float32)
 
     def query_rows(m):
-        return jnp.concatenate([split[m], jnp.zeros((128, BLOCK_ROWS), jnp.bfloat16)], axis=0)
+        gap = jnp.zeros((HEAD_DIM, BLOCK_ROWS), jnp.bfloat16)
+        return jnp.concatenate([split[m, :HEAD_DIM, :], gap, split[m, HEAD_DIM:, :], gap], axis=0)
 
     def exact_query_rows(m):
         halves = [
@@ -315,7 +328,7 @@
 
     def key_rows(kt, part):
         at = pl.multiple_of(kt * KEY_TILE + part * unit, unit)
-        return jnp.concatenate([kvs[pl.ds(at, unit), :], blank], axis=1)
+        return jnp.concatenate([kvs[pl.ds(at, unit), :]] * 2, axis=1)
 
     def value_columns(kt, part):
         return vt[kt, :, part * unit : (part + 1) * unit]
@@ -401,26 +414,15 @@
         pltpu.matmul_acc_lhs(ring(i, 0), jnp.zeros((unit, 256), jnp.bfloat16), load_staged_rhs=0)
         probs[i, :unit] = pltpu.matmul_pop(ring(i, 0)).astype(jnp.bfloat16)
 
-    chunks = sems.shape[0]
-    per_chunk = row_blocks // chunks
-
     def finish(m, worst):
         totals = acc[m, HEAD_DIM : HEAD_DIM + 1, :]
-        staged[m] = (acc[m, :HEAD_DIM, :] * (1.0 / totals)).astype(jnp.bfloat16)
+        out_ref[m] = (acc[m, :HEAD_DIM, :] * (1.0 / totals)).astype(jnp.bfloat16)
         fine = jnp.logical_and(totals > LEAST_TOTAL, totals < MOST_TOTAL)
         return jnp.maximum(worst, jnp.where(fine, 0.0, 1.0))
 
-    def send(c):
-        cut = pl.ds(c * per_chunk, per_chunk)
-        return pltpu.make_async_copy(staged.at[cut], out_ref.at[cut], sems.at[c])
-
     worst = jnp.zeros((1, BLOCK_ROWS), jnp.float32)
-    for c in range(chunks):
-        worst = lax.fori_loop(c * per_chunk, (c + 1) * per_chunk, finish, worst)
-        send(c).start()
+    worst = lax.fori_loop(0, row_blocks // 4, four(finish), worst)
     flag[0] = jnp.max(worst)
-    for c in range(chunks):
-        send(c).wait()
 
     @pl.when(flag[0] > 0.0)
     def _():
@@ -459,14 +461,10 @@
 
             lax.fori_loop(0, key_tiles, fold_sum, 0)
             totals = acc[m, HEAD_DIM : HEAD_DIM + 1, :]
-            staged[m] = (acc[m, :HEAD_DIM, :] * (1.0 / totals)).astype(jnp.bfloat16)
+            out_ref[m] = (acc[m, :HEAD_DIM, :] * (1.0 / totals)).astype(jnp.bfloat16)
             return carry
 
         lax.fori_loop(0, row_blocks, redo, 0)
-        for c in range(chunks):
-            send(c).start()
-        for c in range(chunks):
-            send(c).wait()
 
 
 def attend_call(group, starts, counts, arrived, blocks):
@@ -477,18 +475,16 @@
         functools.partial(attend_kernel, blocks),
         out_shape=jax.ShapeDtypeStruct((row_blocks, HEAD_DIM, BLOCK_ROWS), jnp.bfloat16),
         in_specs=[smem(), smem(), vmem(), vmem()],
-        out_specs=hbm(),
+        out_specs=vmem(),
         scratch_shapes=[
             pltpu.VMEM((patches, 128), jnp.bfloat16),
             pltpu.VMEM((key_tiles, HEAD_DIM + SUM_ROWS, KEY_TILE), jnp.bfloat16),
             pltpu.VMEM((KEY_TILE // 2, 128), jnp.bfloat16),
             pltpu.VMEM((row_blocks + 1, HEAD_DIM + SUM_ROWS, BLOCK_ROWS), jnp.float32),
             pltpu.VMEM((UNROLL, KEY_TILE, BLOCK_ROWS), jnp.bfloat16),
-            pltpu.VMEM((row_blocks, HEAD_DIM, BLOCK_ROWS), jnp.bfloat16),
             pltpu.VMEM((row_blocks, 2 * HEAD_DIM, BLOCK_ROWS), jnp.bfloat16),
             pltpu.SMEM((key_tiles + 2 * UNROLL + 2,), jnp.int32),
             pltpu.SMEM((1,), jnp.float32),
-            pltpu.SemaphoreType.DMA((4,)),
         ],
         compiler_params=pltpu.CompilerParams(vmem_limit_bytes=50 * MIB),
         cost_estimate=pl.CostEstimate(
@@ -500,30 +496,19 @@
     )(group, starts, counts, arrived)
 
 
-OUT_PARTS = 4
-
-
-def out_kernel(h_ref, w_ref, x_ref, gain_ref, out_ref, weights, acc, staged, ins, outs):
+def out_kernel(h_ref, w_ref, x_ref, gain_ref, out_ref, rows_in, staged, ins, outs):
     copies = h_ref.shape[0]
     width = w_ref.shape[0]
-    depth = width // OUT_PARTS
-    loads = []
-    for i in range(OUT_PARTS):
-        cut = pl.ds(i * depth, depth)
-        loads.append(pltpu.make_async_copy(w_ref.at[cut], weights.at[cut], ins.at[i]))
-        loads[i].start()
-    for i in range(OUT_PARTS):
-        loads[i].wait()
-        part = weights[i * depth : (i + 1) * depth, :]
-        heads = depth // HEAD_DIM
-        for r in range(copies):
-            head_out = h_ref[r, i * heads : (i + 1) * heads].reshape(depth, BLOCK_ROWS).T
-            product = jnp.dot(head_out, part, preferred_element_type=jnp.float32)
-            acc[r] = product if i == 0 else acc[r] + product
+    load = pltpu.make_async_copy(x_ref, rows_in, ins.at[0])
+    load.start()
     sent = []
     for r in range(copies):
         cut = slice(r * BLOCK_ROWS, (r + 1) * BLOCK_ROWS)
-        residual = x_ref[cut, :].astype(jnp.float32) + acc[r]
+        head_out = h_ref[r].reshape(width, BLOCK_ROWS).T
+        product = jnp.dot(head_out, w_ref[...], preferred_element_type=jnp.float32)
+        if r == 0:
+            load.wait()
+        residual = rows_in[cut, :].astype(jnp.float32) + product
         staged[cut, :] = norm_rows(residual, gain_ref[...]).astype(jnp.bfloat16)
         where = pl.ds(r * BLOCK_ROWS, BLOCK_ROWS)
         send = pltpu.make_async_copy(staged.at[where], out_ref.at[where], outs.at[r])
@@ -538,13 +523,13 @@
     return pl.pallas_call(
         out_kernel,
         out_shape=jax.ShapeDtypeStruct(x.shape, jnp.bfloat16),
-        in_specs=[vmem(), hbm(), vmem(), vmem()],
+        in_specs=[vmem(), vmem(), hbm(), vmem()],
         out_specs=hbm(),
+        input_output_aliases={2: 0},
         scratch_shapes=[
-            pltpu.VMEM(w_out.shape, jnp.bfloat16),
-            pltpu.VMEM((rows // BLOCK_ROWS, BLOCK_ROWS, width), jnp.float32),
             pltpu.VMEM(x.shape, jnp.bfloat16),
-            pltpu.SemaphoreType.DMA((OUT_PARTS,)),
+            pltpu.VMEM(x.shape, jnp.bfloat16),
+            pltpu.SemaphoreType.DMA((1,)),
             pltpu.SemaphoreType.DMA((rows // BLOCK_ROWS,)),
         ],
         compiler_params=pltpu.CompilerParams(vmem_limit_bytes=50 * MIB),
@@ -570,7 +555,7 @@
     latents = lax.all_to_all(sent, ("seq", "mp"), 0, 0, tiled=True)
     latents = latents.reshape(seqs, mps, part, features)
     lengths = patch_lengths[0].reshape(-1, 128)
-    buf, starts, counts = query_call(x, w_query, lengths, mps * x.shape[0])
+    buf, starts, counts, kept = query_call(x, w_query, lengths, mps * x.shape[0])
 
     buf = kv_call(latents, w_down, kv_gain, w_key, w_value, buf)
     arrived = lax.all_to_all(buf, "mp", 0, 0, tiled=True)
@@ -579,7 +564,7 @@
     head_out = attend_call(group, starts, counts, arrived, seqs)
     head_out = lax.all_to_all(head_out, "mp", 0, 0, tiled=True)
     decoded = out_call(
-        head_out.reshape(copies, HEADS, HEAD_DIM, BLOCK_ROWS), w_out, x, out_gain
+        head_out.reshape(copies, HEADS, HEAD_DIM, BLOCK_ROWS), w_out, kept, out_gain
     )
     return decoded[None]
 

time: 304 us -> 302 us (level)
  no operation moved by 1% of the time
where the time goes in v4:
time: 302 us; the launch traced here: 301 us
  Pallas kernels  217 us (72%)
  waiting for transfers between devices  58.8 us (19%)
  starting transfers between devices  22.2 us (7%)
    pallas_call x1, Pallas kernels, attend_call(): pl.pallas_call(functools.partial(attend_kernel, blocks), out_shape=jax.Sh...  204 us
    all_to_all x1, waiting for transfers between devices, per_device(): arrived = lax.all_to_all(buf, 'mp', 0, 0, tiled=True)  28.7 us
    all_to_all x1, waiting for transfers between devices, per_device(): head_out = lax.all_to_all(head_out, 'mp', 0, 0, tiled=True)  17 us
    all_to_all x1, waiting for transfers between devices, per_device(): latents = lax.all_to_all(sent, ('seq', 'mp'), 0, 0, tiled=True)  13.1 us
    all_to_all x1, starting transfers between devices, per_device(): latents = lax.all_to_all(sent, ('seq', 'mp'), 0, 0, tiled=True)  10.3 us
    pallas_call x1, Pallas kernels, kv_call(): pl.pallas_call(kv_kernel, out_shape=jax.ShapeDtypeStruct(buf.shape, buf.d...  6.38 us
    all_to_all x1, starting transfers between devices, per_device(): head_out = lax.all_to_all(head_out, 'mp', 0, 0, tiled=True)  6.29 us
  transfers between devices with their start and end apart: 3, of which 3 were waited for; matrix products, arithmetic and copies ran while one was open for 0% of the time, Pallas kernels for 1%

profile of v4, /device:TPU:24, one launch (start us, length us, event | category | flops | bytes accessed | tf_op | source)
XLA Modules:
  0.0 301.0 jit_solution(10490636186243693370)
XLA Ops:
  0.0 0.0 copy-start.5
  0.0 0.0 copy-start.3
  0.0 0.0 copy-start.4
  0.0 10.3 %all-to-all-start = ((bf16[128,32,128]{2,1,0:T(8,128)(2,1)}), bf16[128,32,128]{2,1,0:T(8,128)(2,1)S(1)}, u32[]{:S(2)}, u32[]{:S(2)}) async-start(bf16[128,32,128]{2,1,0:T(8,128)(2,1)} %bitcast.11), calls=%async_computation | async-start | bytes 2097152 | tf_op jit(solution)/shard_map/all_to_all | solution.py:555
  10.3 0.0 copy-done.5
  10.3 0.0 copy-done.3
  10.3 0.0 copy-done.4
  10.3 0.0 copy-start.2
  10.3 1.6 copy-done.2
  11.9 3.4 %queries.1 = (bf16[32,256,128]{2,1,0:T(8,128)(2,1)}, s32[32,128]{1,0:T(8,128)S(1)}, s32[128,128]{1,0:T(8,128)S(1)}, bf16[512,1024]{1,0:T(8,128)(2,1)}) custom-call(bf16[512,1024]{1,0:T(8,128)(2,1)S(1)} %bitcast.9, bf16[1024,1024]{1,0:T(8,128)(2,1)S(1)} %copy-done.2, s32[32,128]{1,0:T(8,128)S(1)} %bitcast.10), custom_call_target="tpu_custom_call" | custom-call | flops 1073741824 | bytes 4194304 | tf_op jit(solution)/shard_map/queries/pallas_call | solution.py:113
  15.4 13.1 %all-to-all-done = bf16[128,32,128]{2,1,0:T(8,128)(2,1)S(1)} async-done(((bf16[128,32,128]{2,1,0:T(8,128)(2,1)}), bf16[128,32,128]{2,1,0:T(8,128)(2,1)S(1)}, u32[]{:S(2)}, u32[]{:S(2)}) %all-to-all-start) | async-done | bytes 1048608 | tf_op jit(solution)/shard_map/all_to_all | solution.py:555
  28.5 6.4 %keys_values.1 = bf16[32,256,128]{2,1,0:T(8,128)(2,1)} custom-call(bf16[4,32,32,128]{3,2,1,0:T(8,128)(2,1)S(1)} %bitcast.7, bf16[4096,1024]{1,0:T(8,128)(2,1)} %wd_ref.1, bf16[1,1024]{1,0:T(2,128)(2,1)S(1)} %reshape.17.gain_ref, bf16[1024,1024]{1,0:T(8,128)(2,1)} %wk_ref.1, bf16[1024,1024]{1,0:T(8,128)(2,1)} %wv_ref.1, ...), custom_call_target="tpu_custom_call", output_to_operand_aliasing={{}: (5, {})} | custom-call | flops 1610612736 | bytes 13631488 | tf_op jit(solution)/shard_map/keys_values/pallas_call | solution.py:209
  34.8 5.7 %all-to-all-start.1 = ((bf16[32,256,128]{2,1,0:T(8,128)(2,1)}), bf16[32,256,128]{2,1,0:T(8,128)(2,1)S(1)}, u32[]{:S(2)}, u32[]{:S(2)}) async-start(bf16[32,256,128]{2,1,0:T(8,128)(2,1)} %keys_values.1), calls=%async_computation.1 | async-start | bytes 4194304 | tf_op jit(solution)/shard_map/all_to_all | solution.py:561
  40.5 0.1 pad_add_fusion.refs_0_
  40.6 28.7 %all-to-all-done.1.refs_3_ = bf16[32,256,128]{2,1,0:T(8,128)(2,1)S(1)} async-done(((bf16[32,256,128]{2,1,0:T(8,128)(2,1)}), bf16[32,256,128]{2,1,0:T(8,128)(2,1)S(1)}, u32[]{:S(2)}, u32[]{:S(2)}) %all-to-all-start.1) | async-done | bytes 2097184 | tf_op jit(solution)/shard_map/all_to_all | solution.py:561
  69.3 0.0 copy-start.6
  69.3 204.3 %attend.1 = bf16[32,64,256]{2,1,0:T(8,128)(2,1)S(1)} custom-call(s32[2]{0:T(128)S(1)} %pad_add_fusion.refs_0_, s32[32,128]{1,0:T(8,128)S(1)} %get-tuple-element.9.refs_1_, s32[128,128]{1,0:T(8,128)S(1)} %get-tuple-element.10.refs_2_, bf16[32,256,128]{2,1,0:T(8,128)(2,1)S(1)} %all-to-all-done.1.refs_3_), custom_call_target="tpu_custom_call" | custom-call | flops 8589934592 | bytes 3145728 | tf_op jit(solution)/shard_map/attend/pallas_call | solution.py:474
  273.6 0.0 copy-start.1
  273.6 1.0 copy-done.1
  274.6 6.3 %all-to-all-start.2 = ((bf16[32,64,256]{2,1,0:T(8,128)(2,1)}), bf16[32,64,256]{2,1,0:T(8,128)(2,1)S(1)}, u32[]{:S(2)}, u32[]{:S(2)}) async-start(bf16[32,64,256]{2,1,0:T(8,128)(2,1)} %copy-done.1), calls=%async_computation.2 | async-start | bytes 2097152 | tf_op jit(solution)/shard_map/all_to_all | solution.py:565
  280.9 0.0 copy-done.6
  280.9 17.0 %all-to-all-done.2 = bf16[32,64,256]{2,1,0:T(8,128)(2,1)S(1)} async-done(((bf16[32,64,256]{2,1,0:T(8,128)(2,1)}), bf16[32,64,256]{2,1,0:T(8,128)(2,1)S(1)}, u32[]{:S(2)}, u32[]{:S(2)}) %all-to-all-start.2) | async-done | bytes 1048608 | tf_op jit(solution)/shard_map/all_to_all | solution.py:565
  297.9 0.0 copy-done
  297.9 3.1 %outputs.1 = bf16[512,1024]{1,0:T(8,128)(2,1)} custom-call(bf16[2,16,64,256]{3,2,1,0:T(8,128)(2,1)S(1)} %bitcast.8, bf16[1024,1024]{1,0:T(8,128)(2,1)S(1)} %copy-done, bf16[512,1024]{1,0:T(8,128)(2,1)} %get-tuple-element.12.x_ref, bf16[1,1024]{1,0:T(2,128)(2,1)S(1)} %reshape.19.gain_ref), custom_call_target="tpu_custom_call", output_to_operand_aliasing={{}: (2, {})} | custom-call | flops 1073741824 | bytes 5242880 | tf_op jit(solution)/shard_map/outputs/pallas_call | solution.py:523
  (3 shorter events, 0.0 us)
Async XLA Ops:
  0.0 10.3 %copy-start.5 = (bf16[1024]{0:T(1024)(128)(2,1)S(1)}, bf16[1024]{0:T(1024)(128)(2,1)}, u32[]{:S(2)}) copy-start(bf16[1024]{0:T(1024)(128)(2,1)} %param.14) | copy-start | bytes 6148
  0.0 10.3 %copy-start.3 = (bf16[1,512,1024]{2,1,0:T(8,128)(2,1)S(1)}, bf16[1,512,1024]{2,1,0:T(8,128)(2,1)}, u32[]{:S(2)}) copy-start(bf16[1,512,1024]{2,1,0:T(8,128)(2,1)} %param.10) | copy-start | bytes 3145732
  0.0 10.3 %copy-start.4 = (s32[1,4096]{1,0:T(1,128)S(1)}, s32[1,4096]{1,0:T(1,128)}, u32[]{:S(2)}) copy-start(s32[1,4096]{1,0:T(1,128)} %param.12) | copy-start | bytes 49156
  0.0 28.4 %all-to-all-start = ((bf16[128,32,128]{2,1,0:T(8,128)(2,1)}), bf16[128,32,128]{2,1,0:T(8,128)(2,1)S(1)}, u32[]{:S(2)}, u32[]{:S(2)}) async-start(bf16[128,32,128]{2,1,0:T(8,128)(2,1)} %bitcast.11), calls=%async_computation | async-start | bytes 2097152 | tf_op jit(solution)/shard_map/all_to_all | solution.py:555
  10.3 1.6 copy-start.2
  34.8 34.5 %all-to-all-start.1 = ((bf16[32,256,128]{2,1,0:T(8,128)(2,1)}), bf16[32,256,128]{2,1,0:T(8,128)(2,1)S(1)}, u32[]{:S(2)}, u32[]{:S(2)}) async-start(bf16[32,256,128]{2,1,0:T(8,128)(2,1)} %keys_values.1), calls=%async_computation.1 | async-start | bytes 4194304 | tf_op jit(solution)/shard_map/all_to_all | solution.py:561
  69.3 211.6 %copy-start.6 = (bf16[1024]{0:T(1024)(128)(2,1)S(1)}, bf16[1024]{0:T(1024)(128)(2,1)}, u32[]{:S(2)}) copy-start(bf16[1024]{0:T(1024)(128)(2,1)} %param.19) | copy-start | bytes 6148
  273.6 1.0 copy-start.1
  274.6 23.3 %copy-start = (bf16[1024,1024]{1,0:T(8,128)(2,1)S(1)}, bf16[1024,1024]{1,0:T(8,128)(2,1)}, u32[]{:S(2)}) copy-start(bf16[1024,1024]{1,0:T(8,128)(2,1)} %w_ref.3) | copy-start | bytes 6291460
  274.6 23.3 %all-to-all-start.2 = ((bf16[32,64,256]{2,1,0:T(8,128)(2,1)}), bf16[32,64,256]{2,1,0:T(8,128)(2,1)S(1)}, u32[]{:S(2)}, u32[]{:S(2)}) async-start(bf16[32,64,256]{2,1,0:T(8,128)(2,1)} %copy-done.1), calls=%async_computation.2 | async-start | bytes 2097152 | tf_op jit(solution)/shard_map/all_to_all | solution.py:565

commit v5 on v4

--- a/solution.py
+++ b/solution.py
@@ -11,8 +11,8 @@
 HEADS = 16
 HEAD_DIM = 64
 BLOCK_ROWS = 256
-KEY_TILE = 512
-UNROLL = 6
+KEY_TILE = 256
+UNROLL = 12
 SUM_ROWS = 16
 TO_LOG2 = math.log2(math.e) / math.sqrt(HEAD_DIM)
 SCALE = 1.0 / math.sqrt(HEAD_DIM)
@@ -144,7 +144,7 @@
 
 
 def kv_kernel(
-    x_ref, wd_ref, gain_ref, wk_ref, wv_ref, old_ref, buf_ref, wd, wk, wv, acc, staged, sems, outs
+    x_ref, wd_ref, gain_ref, wk, wv_ref, old_ref, buf_ref, wd, wv, acc, staged, sems, outs
 ):
     blocks, groups, part, lanes = x_ref.shape
     rows = blocks * part
@@ -156,8 +156,7 @@
         )
         for i in range(WD_PARTS)
     ]
-    loads.append(pltpu.make_async_copy(wk_ref, wk, sems.at[WD_PARTS]))
-    loads.append(pltpu.make_async_copy(wv_ref, wv, sems.at[WD_PARTS + 1]))
+    loads.append(pltpu.make_async_copy(wv_ref, wv, sems.at[WD_PARTS]))
     for load in loads[:AHEAD]:
         load.start()
     for i in range(WD_PARTS):
@@ -177,9 +176,8 @@
     copies = buf_ref.shape[0] // HEADS
     step = 256
     heads_step = step // HEAD_DIM
+    acc[...] = jnp.dot(normed, wk[...], preferred_element_type=jnp.float32)
     loads[WD_PARTS].wait()
-    acc[...] = jnp.dot(normed, wk[...], preferred_element_type=jnp.float32)
-    loads[WD_PARTS + 1].wait()
     sent = []
     for n in range(wv.shape[1] // step):
         cut = slice(n * step, (n + 1) * step)
@@ -209,19 +207,18 @@
     return pl.pallas_call(
         kv_kernel,
         out_shape=jax.ShapeDtypeStruct(buf.shape, buf.dtype),
-        in_specs=[vmem(), hbm(), vmem(), hbm(), hbm(), hbm()],
+        in_specs=[vmem(), hbm(), vmem(), vmem(), hbm(), hbm()],
         out_specs=hbm(),
         input_output_aliases={5: 0},
         scratch_shapes=[
             pltpu.VMEM(w_down.shape, jnp.bfloat16),
-            pltpu.VMEM(w_key.shape, jnp.bfloat16),
             pltpu.VMEM(w_value.shape, jnp.bfloat16),
             pltpu.VMEM((rows, width), jnp.float32),
             pltpu.VMEM((HEADS, rows, 2 * HEAD_DIM), jnp.bfloat16),
-            pltpu.SemaphoreType.DMA((WD_PARTS + 2,)),
+            pltpu.SemaphoreType.DMA((WD_PARTS + 1,)),
             pltpu.SemaphoreType.DMA((buf.shape[0] // HEADS * width // 256,)),
         ],
-        compiler_params=pltpu.CompilerParams(vmem_limit_bytes=50 * MIB),
+        compiler_params=pltpu.CompilerParams(vmem_limit_bytes=47 * MIB),
         cost_estimate=pl.CostEstimate(
             flops=2 * rows * width * (groups * lanes + 2 * width),
             bytes_accessed=2 * (rows * groups * lanes + groups * lanes * width + 2 * width * width),
@@ -236,7 +233,7 @@
 
 
 def attend_kernel(blocks, *refs):
-    unit = KEY_TILE // 2
+    unit = KEY_TILE
     kinds = []
     for mxu in range(2):
         kinds += [pltpu.ACC(mxu)((unit, BLOCK_ROWS), jnp.float32)] * 3
@@ -248,7 +245,7 @@
     group_ref, starts_ref, counts_ref, in_ref, out_ref = refs[:5]
     kvs, vt, order, acc, probs, split, lows, flag = refs[5:]
     score_accs, sum_accs = (accs[0:3], accs[6:9]), (accs[3:6], accs[9:12])
-    unit = KEY_TILE // 2
+    unit = KEY_TILE
     row_blocks = in_ref.shape[0]
     senders = row_blocks
     part = 128 // blocks
@@ -321,17 +318,14 @@
         met = [counts_ref[pl.ds(line + b, 1), :] for b in range(lanes)]
         return jnp.concatenate(met, axis=1)
 
-    def allowed_keys(m, kt, part):
-        met = jnp.clip(last_keys(m) - (kt * KEY_TILE + part * unit), 0, unit)
+    def allowed_keys(m, kt):
+        met = jnp.clip(last_keys(m) - kt * KEY_TILE, 0, unit)
         met = met.astype(jnp.float32).astype(jnp.bfloat16)
         return jnp.concatenate([order[...]] * lanes, axis=1) < met
 
-    def key_rows(kt, part):
-        at = pl.multiple_of(kt * KEY_TILE + part * unit, unit)
+    def key_rows(kt):
+        at = pl.multiple_of(kt * KEY_TILE, unit)
         return jnp.concatenate([kvs[pl.ds(at, unit), :]] * 2, axis=1)
-
-    def value_columns(kt, part):
-        return vt[kt, :, part * unit : (part + 1) * unit]
 
     def inside(kt, m):
         return jnp.minimum(kt, key_tiles - 1), jnp.minimum(m, row_blocks - 1)
@@ -341,16 +335,15 @@
         kt = kt + wrap.astype(jnp.int32)
         return kt, jnp.where(wrap, lows[kt], m + 1)
 
-    def ring(i, part):
-        return score_accs[i % 2][(2 * (i // 2) + part) % 3]
+    def ring(i):
+        return score_accs[i % 2][(i // 2) % 3]
 
     def total_of(i):
         return sum_accs[i % 2][(i // 2) % 3]
 
-    def settle_scores(i, part, kt, m):
-        p = jnp.exp2(pltpu.matmul_pop(ring(i, part))).astype(jnp.bfloat16)
-        p = jnp.where(allowed_keys(m, kt, part), p, jnp.zeros_like(p))
-        probs[i, part * unit : (part + 1) * unit] = p
+    def settle_scores(i, kt, m):
+        p = jnp.exp2(pltpu.matmul_pop(ring(i))).astype(jnp.bfloat16)
+        probs[i] = jnp.where(allowed_keys(m, kt), p, jnp.zeros_like(p))
 
     def settle_sums(i, m):
         acc[m] = acc[m] + pltpu.matmul_pop(total_of(i))
@@ -359,6 +352,8 @@
         for mxu in range(2):
             stage(query_rows(inside(kt, m)[1]), 0, mxu)
             kt, m = advance(kt, m)
+
+    left = range(UNROLL - 4, UNROLL)
 
     def body(_, carry):
         kt, m, old, open_sums = carry
@@ -368,33 +363,26 @@
             kt, m = advance(kt, m)
         for j in range(0, UNROLL, 2):
             now = (j, j + 1)
-            if j == 0:
+            if j < 4:
                 before = [
-                    (i, old[3 * i], old[3 * i + 1], open_sums[i - UNROLL + 2])
-                    for i in (UNROLL - 2, UNROLL - 1)
+                    (i, old[3 * i], old[3 * i + 1], open_sums[i - UNROLL + 4])
+                    for i in (UNROLL - 4 + j, UNROLL - 3 + j)
                 ]
             else:
-                before = [(i, pairs[i][0], pairs[i][1], old[3 * i + 2]) for i in (j - 2, j - 1)]
+                before = [(i, pairs[i][0], pairs[i][1], old[3 * i + 2]) for i in (j - 4, j - 3)]
             for i in now:
-                pltpu.matmul_acc_lhs(ring(i, 0), key_rows(pairs[i][0], 0), load_staged_rhs=0)
-                stage(probs[i, :unit], 0, i % 2)
-                stage(probs[i, unit:], 1, i % 2)
-            for i, b_kt, b_m, _ in before:
-                settle_scores(i, 0, b_kt, b_m)
-            for i in now:
-                pltpu.matmul_acc_lhs(ring(i, 1), key_rows(pairs[i][0], 1))
-            for i, b_kt, b_m, _ in before:
-                settle_scores(i, 1, b_kt, b_m)
-            for i in now:
-                old_kt = old[3 * i]
-                pltpu.matmul_acc_lhs(total_of(i), value_columns(old_kt, 0), load_staged_rhs=0)
+                pltpu.matmul_acc_lhs(ring(i), key_rows(pairs[i][0]), load_staged_rhs=0)
+                stage(probs[i], 1, i % 2)
                 if i + 2 < UNROLL:
                     stage(query_rows(pairs[i + 2][1]), 0, i % 2)
-                pltpu.matmul_acc_lhs(total_of(i), value_columns(old_kt, 1), load_staged_rhs=1)
+            for i, b_kt, b_m, _ in before:
+                settle_scores(i, b_kt, b_m)
+            for i in now:
+                pltpu.matmul_acc_lhs(total_of(i), vt[old[3 * i]], load_staged_rhs=1)
             for i, _, _, b_m in before:
                 settle_sums(i, b_m)
         stage_first(kt, m)
-        now_open = tuple(old[3 * i + 2] for i in (UNROLL - 2, UNROLL - 1))
+        now_open = tuple(old[3 * i + 2] for i in left)
         return kt, m, tuple(v for pair in pairs for v in pair), now_open
 
     trash = jnp.int32(row_blocks)
@@ -404,15 +392,13 @@
         probs[0, : spare.shape[0]] = pltpu.matmul_pop(spare).astype(jnp.bfloat16)
     first = (jnp.int32(0), lows[0])
     stage_first(*first)
-    kt, m, _, open_sums = lax.fori_loop(0, steps, body, first + (nothing, (trash, trash)))
-    for i in (UNROLL - 2, UNROLL - 1):
-        settle_sums(i, open_sums[i - UNROLL + 2])
-        for part in range(2):
-            probs[i, part * unit : (part + 1) * unit] = pltpu.matmul_pop(ring(i, part)).astype(
-                jnp.bfloat16
-            )
-        pltpu.matmul_acc_lhs(ring(i, 0), jnp.zeros((unit, 256), jnp.bfloat16), load_staged_rhs=0)
-        probs[i, :unit] = pltpu.matmul_pop(ring(i, 0)).astype(jnp.bfloat16)
+    kt, m, _, open_sums = lax.fori_loop(0, steps, body, first + (nothing, (trash,) * 4))
+    for i in left:
+        settle_sums(i, open_sums[i - UNROLL + 4])
+        probs[i] = pltpu.matmul_pop(ring(i)).astype(jnp.bfloat16)
+    for i in (0, 1):
+        pltpu.matmul_acc_lhs(ring(i), jnp.zeros((unit, 256), jnp.bfloat16), load_staged_rhs=0)
+        probs[i] = pltpu.matmul_pop(ring(i)).astype(jnp.bfloat16)
 
     def finish(m, worst):
         totals = acc[m, HEAD_DIM : HEAD_DIM + 1, :]
@@ -429,20 +415,15 @@
         def redo(m, carry):
             def masked_scores(kt):
                 stage(exact_query_rows(m), 0, 0)
-                pltpu.matmul_acc_lhs(score_accs[0][0], key_rows(kt, 0), load_staged_rhs=0)
-                pltpu.matmul_acc_lhs(score_accs[0][1], key_rows(kt, 1))
-                parts = []
-                for part in range(2):
-                    scores = pltpu.matmul_pop(score_accs[0][part]) * SCALE
-                    met = jnp.clip(last_keys(m) - (kt * KEY_TILE + part * unit), 0, unit)
-                    parts.append((scores, iota((unit, BLOCK_ROWS), 0) < met))
-                return parts
+                pltpu.matmul_acc_lhs(score_accs[0][0], key_rows(kt), load_staged_rhs=0)
+                scores = pltpu.matmul_pop(score_accs[0][0]) * SCALE
+                met = jnp.clip(last_keys(m) - kt * KEY_TILE, 0, unit)
+                return scores, iota((unit, BLOCK_ROWS), 0) < met
 
             def fold_max(kt, peak):
-                for scores, allowed in masked_scores(kt):
-                    masked = jnp.where(allowed, scores, -3e38)
-                    peak = jnp.maximum(peak, jnp.max(masked, axis=0, keepdims=True))
-                return peak
+                scores, allowed = masked_scores(kt)
+                masked = jnp.where(allowed, scores, -3e38)
+                return jnp.maximum(peak, jnp.max(masked, axis=0, keepdims=True))
 
             peak = lax.fori_loop(
                 0, key_tiles, fold_max, jnp.full((1, BLOCK_ROWS), -3e38, jnp.float32)
@@ -450,12 +431,10 @@
             acc[m] = jnp.zeros(acc.shape[1:], jnp.float32)
 
             def fold_sum(kt, inner):
-                for part, (scores, allowed) in enumerate(masked_scores(kt)):
-                    p = jnp.where(allowed, jnp.exp(jnp.where(allowed, scores - peak, 0.0)), 0.0)
-                    stage(p.astype(jnp.bfloat16), 0, 0)
-                    pltpu.matmul_acc_lhs(
-                        sum_accs[0][0], value_columns(kt, part), load_staged_rhs=0
-                    )
+                scores, allowed = masked_scores(kt)
+                p = jnp.where(allowed, jnp.exp(jnp.where(allowed, scores - peak, 0.0)), 0.0)
+                stage(p.astype(jnp.bfloat16), 0, 0)
+                pltpu.matmul_acc_lhs(sum_accs[0][0], vt[kt], load_staged_rhs=0)
                 acc[m] = acc[m] + pltpu.matmul_pop(sum_accs[0][0])
                 return inner
 
@@ -479,7 +458,7 @@
         scratch_shapes=[
             pltpu.VMEM((patches, 128), jnp.bfloat16),
             pltpu.VMEM((key_tiles, HEAD_DIM + SUM_ROWS, KEY_TILE), jnp.bfloat16),
-            pltpu.VMEM((KEY_TILE // 2, 128), jnp.bfloat16),
+            pltpu.VMEM((KEY_TILE, 128), jnp.bfloat16),
             pltpu.VMEM((row_blocks + 1, HEAD_DIM + SUM_ROWS, BLOCK_ROWS), jnp.float32),
             pltpu.VMEM((UNROLL, KEY_TILE, BLOCK_ROWS), jnp.bfloat16),
             pltpu.VMEM((row_blocks, 2 * HEAD_DIM, BLOCK_ROWS), jnp.bfloat16),

time: 302 us -> 418 us (1.38)
  Pallas kernels: 217 us -> 333 us
    pallas_call x1, Pallas kernels: 204 us -> 321 us  [attend_call(): pl.pallas_call(functools.partial(attend_kernel, blocks), out_shape=jax.Sh...]
where the time goes in v5:
time: 418 us; the launch traced here: 416 us
  Pallas kernels  333 us (80%)
  waiting for transfers between devices  57.2 us (14%)
  starting transfers between devices  21.9 us (5%)
    pallas_call x1, Pallas kernels, attend_call(): pl.pallas_call(functools.partial(attend_kernel, blocks), out_shape=jax.Sh...  321 us
    all_to_all x1, waiting for transfers between devices, per_device(): arrived = lax.all_to_all(buf, 'mp', 0, 0, tiled=True)  28.7 us
    all_to_all x1, waiting for transfers between devices, per_device(): head_out = lax.all_to_all(head_out, 'mp', 0, 0, tiled=True)  16.8 us
    all_to_all x1, waiting for transfers between devices, per_device(): latents = lax.all_to_all(sent, ('seq', 'mp'), 0, 0, tiled=True)  11.7 us
    all_to_all x1, starting transfers between devices, per_device(): latents = lax.all_to_all(sent, ('seq', 'mp'), 0, 0, tiled=True)  10.3 us
  transfers between devices with their start and end apart: 3, of which 3 were waited for; matrix products, arithmetic and copies ran while one was open for 0% of the time, Pallas kernels for 1%

profile of v5, /device:TPU:24, one launch (start us, length us, event | category | flops | bytes accessed | tf_op | source)
XLA Modules:
  0.0 416.3 jit_solution(1207723899552968994)
XLA Ops:
  0.0 0.0 copy-start.6
  0.0 0.0 copy-start.5
  0.0 10.3 %all-to-all-start = ((bf16[128,32,128]{2,1,0:T(8,128)(2,1)}), bf16[128,32,128]{2,1,0:T(8,128)(2,1)S(1)}, u32[]{:S(2)}, u32[]{:S(2)}) async-start(bf16[128,32,128]{2,1,0:T(8,128)(2,1)} %bitcast.11), calls=%async_computation | async-start | bytes 2097152 | tf_op jit(solution)/shard_map/all_to_all | solution.py:534
  10.3 0.0 copy-done.6
  10.3 0.0 copy-start
  10.3 0.0 copy-done.5
  10.3 0.0 copy-start.3
  10.3 1.7 copy-done.3
  12.1 1.2 copy-done.4
  13.3 3.4 queries.1
  16.7 11.7 %all-to-all-done = bf16[128,32,128]{2,1,0:T(8,128)(2,1)S(1)} async-done(((bf16[128,32,128]{2,1,0:T(8,128)(2,1)}), bf16[128,32,128]{2,1,0:T(8,128)(2,1)S(1)}, u32[]{:S(2)}, u32[]{:S(2)}) %all-to-all-start) | async-done | bytes 1048608 | tf_op jit(solution)/shard_map/all_to_all | solution.py:534
  28.4 0.0 copy-done
  28.4 6.0 %keys_values.1 = bf16[32,256,128]{2,1,0:T(8,128)(2,1)} custom-call(bf16[4,32,32,128]{3,2,1,0:T(8,128)(2,1)S(1)} %bitcast.7, bf16[4096,1024]{1,0:T(8,128)(2,1)} %wd_ref.1, bf16[1,1024]{1,0:T(2,128)(2,1)S(1)} %reshape.17.gain_ref, bf16[1024,1024]{1,0:T(8,128)(2,1)S(1)} %copy-done, bf16[1024,1024]{1,0:T(8,128)(2,1)} %wv_ref.1, ...), custom_call_target="tpu_custom_call", output_to_operand_aliasing={{}: (5, {})} | custom-call | flops 1610612736 | bytes 13631488 | tf_op jit(solution)/shard_map/keys_values/pallas_call | solution.py:207
  34.4 5.7 %all-to-all-start.1 = ((bf16[32,256,128]{2,1,0:T(8,128)(2,1)}), bf16[32,256,128]{2,1,0:T(8,128)(2,1)S(1)}, u32[]{:S(2)}, u32[]{:S(2)}) async-start(bf16[32,256,128]{2,1,0:T(8,128)(2,1)} %keys_values.1), calls=%async_computation.1 | async-start | bytes 4194304 | tf_op jit(solution)/shard_map/all_to_all | solution.py:540
  40.1 0.1 pad_add_fusion.refs_0_
  40.2 28.7 %all-to-all-done.1.refs_3_ = bf16[32,256,128]{2,1,0:T(8,128)(2,1)S(1)} async-done(((bf16[32,256,128]{2,1,0:T(8,128)(2,1)}), bf16[32,256,128]{2,1,0:T(8,128)(2,1)S(1)}, u32[]{:S(2)}, u32[]{:S(2)}) %all-to-all-start.1) | async-done | bytes 2097184 | tf_op jit(solution)/shard_map/all_to_all | solution.py:540
  68.9 320.6 %attend.1 = bf16[32,64,256]{2,1,0:T(8,128)(2,1)S(1)} custom-call(s32[2]{0:T(128)S(1)} %pad_add_fusion.refs_0_, s32[32,128]{1,0:T(8,128)S(1)} %get-tuple-element.9.refs_1_, s32[128,128]{1,0:T(8,128)S(1)} %get-tuple-element.10.refs_2_, bf16[32,256,128]{2,1,0:T(8,128)(2,1)S(1)} %all-to-all-done.1.refs_3_), custom_call_target="tpu_custom_call" | custom-call | flops 8589934592 | bytes 3145728 | tf_op jit(solution)/shard_map/attend/pallas_call | solution.py:453
  389.5 0.0 copy-start.2
  389.5 1.0 copy-done.2
  390.5 5.9 %all-to-all-start.2 = ((bf16[32,64,256]{2,1,0:T(8,128)(2,1)}), bf16[32,64,256]{2,1,0:T(8,128)(2,1)S(1)}, u32[]{:S(2)}, u32[]{:S(2)}) async-start(bf16[32,64,256]{2,1,0:T(8,128)(2,1)} %copy-done.2), calls=%async_computation.2 | async-start | bytes 2097152 | tf_op jit(solution)/shard_map/all_to_all | solution.py:544
  396.4 0.0 copy-done.7
  396.4 16.8 %all-to-all-done.2 = bf16[32,64,256]{2,1,0:T(8,128)(2,1)S(1)} async-done(((bf16[32,64,256]{2,1,0:T(8,128)(2,1)}), bf16[32,64,256]{2,1,0:T(8,128)(2,1)S(1)}, u32[]{:S(2)}, u32[]{:S(2)}) %all-to-all-start.2) | async-done | bytes 1048608 | tf_op jit(solution)/shard_map/all_to_all | solution.py:544
  413.2 0.0 copy-done.1
  413.2 3.1 outputs.1
  (5 shorter events, 0.0 us)
Async XLA Ops:
  0.0 10.3 %copy-start.6 = (bf16[1024]{0:T(1024)(128)(2,1)S(1)}, bf16[1024]{0:T(1024)(128)(2,1)}, u32[]{:S(2)}) copy-start(bf16[1024]{0:T(1024)(128)(2,1)} %param.14) | copy-start | bytes 6148
  0.0 10.3 %copy-start.5 = (s32[1,4096]{1,0:T(1,128)S(1)}, s32[1,4096]{1,0:T(1,128)}, u32[]{:S(2)}) copy-start(s32[1,4096]{1,0:T(1,128)} %param.12) | copy-start | bytes 49156
  0.0 28.4 %all-to-all-start = ((bf16[128,32,128]{2,1,0:T(8,128)(2,1)}), bf16[128,32,128]{2,1,0:T(8,128)(2,1)S(1)}, u32[]{:S(2)}, u32[]{:S(2)}) async-start(bf16[128,32,128]{2,1,0:T(8,128)(2,1)} %bitcast.11), calls=%async_computation | async-start | bytes 2097152 | tf_op jit(solution)/shard_map/all_to_all | solution.py:534
  10.3 18.2 %copy-start = (bf16[1024,1024]{1,0:T(8,128)(2,1)S(1)}, bf16[1024,1024]{1,0:T(8,128)(2,1)}, u32[]{:S(2)}) copy-start(bf16[1024,1024]{1,0:T(8,128)(2,1)} %wk.1) | copy-start | bytes 6291460
  10.3 1.7 copy-start.3
  12.1 1.2 copy-start.4
  34.4 34.5 %all-to-all-start.1 = ((bf16[32,256,128]{2,1,0:T(8,128)(2,1)}), bf16[32,256,128]{2,1,0:T(8,128)(2,1)S(1)}, u32[]{:S(2)}, u32[]{:S(2)}) async-start(bf16[32,256,128]{2,1,0:T(8,128)(2,1)} %keys_values.1), calls=%async_computation.1 | async-start | bytes 4194304 | tf_op jit(solution)/shard_map/all_to_all | solution.py:540
  68.9 327.5 %copy-start.7 = (bf16[1024]{0:T(1024)(128)(2,1)S(1)}, bf16[1024]{0:T(1024)(128)(2,1)}, u32[]{:S(2)}) copy-start(bf16[1024]{0:T(1024)(128)(2,1)} %param.19) | copy-start | bytes 6148
  389.5 1.0 copy-start.2
  390.5 22.7 %copy-start.1 = (bf16[1024,1024]{1,0:T(8,128)(2,1)S(1)}, bf16[1024,1024]{1,0:T(8,128)(2,1)}, u32[]{:S(2)}) copy-start(bf16[1024,1024]{1,0:T(8,128)(2,1)} %w_ref.3) | copy-start | bytes 6291460
  390.5 22.7 %all-to-all-start.2 = ((bf16[32,64,256]{2,1,0:T(8,128)(2,1)}), bf16[32,64,256]{2,1,0:T(8,128)(2,1)S(1)}, u32[]{:S(2)}, u32[]{:S(2)}) async-start(bf16[32,64,256]{2,1,0:T(8,128)(2,1)} %copy-done.2), calls=%async_computation.2 | async-start | bytes 2097152 | tf_op jit(solution)/shard_map/all_to_all | solution.py:544

commit v6 on v5

--- a/solution.py
+++ b/solution.py
@@ -140,7 +140,7 @@
 
 
 WD_PARTS = 8
-AHEAD = 5
+AHEAD = 7
 
 
 def kv_kernel(

time: 418 us -> 418 us (level)
  no operation moved by 1% of the time
where the time goes in v6:
time: 418 us; the launch traced here: 417 us
  Pallas kernels  333 us (80%)
  waiting for transfers between devices  57.8 us (14%)
  starting transfers between devices  21.9 us (5%)
    pallas_call x1, Pallas kernels, attend_call(): pl.pallas_call(functools.partial(attend_kernel, blocks), out_shape=jax.Sh...  321 us
    all_to_all x1, waiting for transfers between devices, per_device(): arrived = lax.all_to_all(buf, 'mp', 0, 0, tiled=True)  28.7 us
    all_to_all x1, waiting for transfers between devices, per_device(): head_out = lax.all_to_all(head_out, 'mp', 0, 0, tiled=True)  17.4 us
    all_to_all x1, waiting for transfers between devices, per_device(): latents = lax.all_to_all(sent, ('seq', 'mp'), 0, 0, tiled=True)  11.7 us
    all_to_all x1, starting transfers between devices, per_device(): latents = lax.all_to_all(sent, ('seq', 'mp'), 0, 0, tiled=True)  10.3 us
  transfers between devices with their start and end apart: 3, of which 3 were waited for; matrix products, arithmetic and copies ran while one was open for 0% of the time, Pallas kernels for 1%

profile of v6, /device:TPU:24, one launch (start us, length us, event | category | flops | bytes accessed | tf_op | source)
XLA Modules:
  0.0 416.8 jit_solution(76348943086992644)
XLA Ops:
  0.0 0.0 copy-start.6
  0.0 0.0 copy-start.5
  0.0 10.3 %all-to-all-start = ((bf16[128,32,128]{2,1,0:T(8,128)(2,1)}), bf16[128,32,128]{2,1,0:T(8,128)(2,1)S(1)}, u32[]{:S(2)}, u32[]{:S(2)}) async-start(bf16[128,32,128]{2,1,0:T(8,128)(2,1)} %bitcast.11), calls=%async_computation | async-start | bytes 2097152 | tf_op jit(solution)/shard_map/all_to_all | solution.py:534
  10.3 0.0 copy-done.6
  10.3 0.0 copy-start
  10.3 0.0 copy-done.5
  10.3 0.0 copy-start.3
  10.3 1.7 copy-done.3
  12.1 1.2 copy-done.4
  13.3 3.4 queries.1
  16.7 11.7 %all-to-all-done = bf16[128,32,128]{2,1,0:T(8,128)(2,1)S(1)} async-done(((bf16[128,32,128]{2,1,0:T(8,128)(2,1)}), bf16[128,32,128]{2,1,0:T(8,128)(2,1)S(1)}, u32[]{:S(2)}, u32[]{:S(2)}) %all-to-all-start) | async-done | bytes 1048608 | tf_op jit(solution)/shard_map/all_to_all | solution.py:534
  28.4 0.0 copy-done
  28.4 5.9 %keys_values.1 = bf16[32,256,128]{2,1,0:T(8,128)(2,1)} custom-call(bf16[4,32,32,128]{3,2,1,0:T(8,128)(2,1)S(1)} %bitcast.7, bf16[4096,1024]{1,0:T(8,128)(2,1)} %wd_ref.1, bf16[1,1024]{1,0:T(2,128)(2,1)S(1)} %reshape.17.gain_ref, bf16[1024,1024]{1,0:T(8,128)(2,1)S(1)} %copy-done, bf16[1024,1024]{1,0:T(8,128)(2,1)} %wv_ref.1, ...), custom_call_target="tpu_custom_call", output_to_operand_aliasing={{}: (5, {})} | custom-call | flops 1610612736 | bytes 13631488 | tf_op jit(solution)/shard_map/keys_values/pallas_call | solution.py:207
  34.3 5.7 %all-to-all-start.1 = ((bf16[32,256,128]{2,1,0:T(8,128)(2,1)}), bf16[32,256,128]{2,1,0:T(8,128)(2,1)S(1)}, u32[]{:S(2)}, u32[]{:S(2)}) async-start(bf16[32,256,128]{2,1,0:T(8,128)(2,1)} %keys_values.1), calls=%async_computation.1 | async-start | bytes 4194304 | tf_op jit(solution)/shard_map/all_to_all | solution.py:540
  40.0 0.1 pad_add_fusion.refs_0_
  40.1 28.7 %all-to-all-done.1.refs_3_ = bf16[32,256,128]{2,1,0:T(8,128)(2,1)S(1)} async-done(((bf16[32,256,128]{2,1,0:T(8,128)(2,1)}), bf16[32,256,128]{2,1,0:T(8,128)(2,1)S(1)}, u32[]{:S(2)}, u32[]{:S(2)}) %all-to-all-start.1) | async-done | bytes 2097184 | tf_op jit(solution)/shard_map/all_to_all | solution.py:540
  68.8 320.6 %attend.1 = bf16[32,64,256]{2,1,0:T(8,128)(2,1)S(1)} custom-call(s32[2]{0:T(128)S(1)} %pad_add_fusion.refs_0_, s32[32,128]{1,0:T(8,128)S(1)} %get-tuple-element.9.refs_1_, s32[128,128]{1,0:T(8,128)S(1)} %get-tuple-element.10.refs_2_, bf16[32,256,128]{2,1,0:T(8,128)(2,1)S(1)} %all-to-all-done.1.refs_3_), custom_call_target="tpu_custom_call" | custom-call | flops 8589934592 | bytes 3145728 | tf_op jit(solution)/shard_map/attend/pallas_call | solution.py:453
  389.4 0.0 copy-start.2
  389.4 1.0 copy-done.2
  390.4 5.9 %all-to-all-start.2 = ((bf16[32,64,256]{2,1,0:T(8,128)(2,1)}), bf16[32,64,256]{2,1,0:T(8,128)(2,1)S(1)}, u32[]{:S(2)}, u32[]{:S(2)}) async-start(bf16[32,64,256]{2,1,0:T(8,128)(2,1)} %copy-done.2), calls=%async_computation.2 | async-start | bytes 2097152 | tf_op jit(solution)/shard_map/all_to_all | solution.py:544
  396.3 0.0 copy-done.7
  396.3 17.4 %all-to-all-done.2 = bf16[32,64,256]{2,1,0:T(8,128)(2,1)S(1)} async-done(((bf16[32,64,256]{2,1,0:T(8,128)(2,1)}), bf16[32,64,256]{2,1,0:T(8,128)(2,1)S(1)}, u32[]{:S(2)}, u32[]{:S(2)}) %all-to-all-start.2) | async-done | bytes 1048608 | tf_op jit(solution)/shard_map/all_to_all | solution.py:544
  413.7 0.0 copy-done.1
  413.7 3.1 outputs.1
  (5 shorter events, 0.0 us)
Async XLA Ops:
  0.0 10.3 %copy-start.6 = (bf16[1024]{0:T(1024)(128)(2,1)S(1)}, bf16[1024]{0:T(1024)(128)(2,1)}, u32[]{:S(2)}) copy-start(bf16[1024]{0:T(1024)(128)(2,1)} %param.14) | copy-start | bytes 6148
  0.0 10.3 %copy-start.5 = (s32[1,4096]{1,0:T(1,128)S(1)}, s32[1,4096]{1,0:T(1,128)}, u32[]{:S(2)}) copy-start(s32[1,4096]{1,0:T(1,128)} %param.12) | copy-start | bytes 49156
  0.0 28.4 %all-to-all-start = ((bf16[128,32,128]{2,1,0:T(8,128)(2,1)}), bf16[128,32,128]{2,1,0:T(8,128)(2,1)S(1)}, u32[]{:S(2)}, u32[]{:S(2)}) async-start(bf16[128,32,128]{2,1,0:T(8,128)(2,1)} %bitcast.11), calls=%async_computation | async-start | bytes 2097152 | tf_op jit(solution)/shard_map/all_to_all | solution.py:534
  10.3 18.2 %copy-start = (bf16[1024,1024]{1,0:T(8,128)(2,1)S(1)}, bf16[1024,1024]{1,0:T(8,128)(2,1)}, u32[]{:S(2)}) copy-start(bf16[1024,1024]{1,0:T(8,128)(2,1)} %wk.1) | copy-start | bytes 6291460
  10.3 1.7 copy-start.3
  12.1 1.2 copy-start.4
  34.3 34.5 %all-to-all-start.1 = ((bf16[32,256,128]{2,1,0:T(8,128)(2,1)}), bf16[32,256,128]{2,1,0:T(8,128)(2,1)S(1)}, u32[]{:S(2)}, u32[]{:S(2)}) async-start(bf16[32,256,128]{2,1,0:T(8,128)(2,1)} %keys_values.1), calls=%async_computation.1 | async-start | bytes 4194304 | tf_op jit(solution)/shard_map/all_to_all | solution.py:540
  68.8 327.5 %copy-start.7 = (bf16[1024]{0:T(1024)(128)(2,1)S(1)}, bf16[1024]{0:T(1024)(128)(2,1)}, u32[]{:S(2)}) copy-start(bf16[1024]{0:T(1024)(128)(2,1)} %param.19) | copy-start | bytes 6148
  389.4 1.0 copy-start.2
  390.4 23.4 %copy-start.1 = (bf16[1024,1024]{1,0:T(8,128)(2,1)S(1)}, bf16[1024,1024]{1,0:T(8,128)(2,1)}, u32[]{:S(2)}) copy-start(bf16[1024,1024]{1,0:T(8,128)(2,1)} %w_ref.3) | copy-start | bytes 6291460
  390.4 23.4 %all-to-all-start.2 = ((bf16[32,64,256]{2,1,0:T(8,128)(2,1)}), bf16[32,64,256]{2,1,0:T(8,128)(2,1)S(1)}, u32[]{:S(2)}, u32[]{:S(2)}) async-start(bf16[32,64,256]{2,1,0:T(8,128)(2,1)} %copy-done.2), calls=%async_computation.2 | async-start | bytes 2097152 | tf_op jit(solution)/shard_map/all_to_all | solution.py:544
